TPU v7x, 256 devices: a whole 4x4x8 slice. The times are simulated.
256 devices in a mesh: dp: 16 (over y_hi, x, core), mp: 16 (over y_lo, z).
Axes of the slice: x: 4, y: 4 (y_hi: 2, y_lo: 2; y = y_hi * 2 + y_lo), z: 8, core: 2. Of those that a mesh axis runs over, the one named last changes fastest.
Arguments:
- grid_latent: bfloat16 [16, 4096, 1024], P('dp', 'mp'), may hold values from -6 to 6
- mesh_latent: bfloat16 [16, 2048, 1024], P('dp', 'mp'), may hold values from -6 to 6
- edge_source: int32 [16, 12288], P('dp', 'mp'), may hold values from 0 to 4095, as said below
- edge_dest: int32 [16, 12288], P('dp', 'mp'), may hold values from 0 to 2047, as said below
- edge_count: int32 [16, 16], P('dp', 'mp'), may hold values from 256 to 768, as said below
- edge_attr: float32 [16, 4, 12288], P('dp', None, 'mp'), may hold values from -5 to 5
- w_attr: float32 [4, 1024], replicated, may hold values from -3 to 3
- w_in: bfloat16 [1024, 1024], replicated, may hold values from -0.1875 to 0.1875
- w_out: bfloat16 [1024, 1024], replicated, may hold values from -0.1875 to 0.1875
- w_qkv: bfloat16 [3, 1024, 1024], P(None, None, 'mp')
- w_o: bfloat16 [1024, 1024], P('mp'), may hold values from -0.1875 to 0.1875
- cotangent: bfloat16 [16, 2048, 1024], P('dp', 'mp'), may hold values from -6 to 6
Outputs:
- d_grid: bfloat16 [16, 4096, 1024], P('dp', 'mp')
- d_mesh: bfloat16 [16, 2048, 1024], P('dp', 'mp')
- d_w_attr: float32 [4, 1024], replicated
- d_w_in: float32 [1024, 1024], P('dp', 'mp')
- d_w_out: float32 [1024, 1024], P('dp', 'mp')
- d_w_qkv: float32 [3, 1024, 1024], P(None, 'dp', 'mp')
- d_w_o: float32 [1024, 1024], P('mp', 'dp')
Inputs may be any that keep to these rules, and one draw needn't show every extreme that they name: `edge_source`: edge slots of band b (positions b * 768 to (b + 1) * 768 - 1 of a sample) name grid points of band b, rows b * 256 to (b + 1) * 256 - 1. `edge_dest`: edge slots of band b name mesh nodes of band b - 1, b or b + 1 (bands of 128 nodes each). `edge_count`: the first and last bands of every sample are full.
All inputs are finite; a program needn't handle non-finite values.
Results may differ from a plain program's by a relative error of at most 0.025.
Values may be sent and summed in bfloat16 or wider, within the bound.
No kernel may reach another device: no remote copies, remote signals or barrier semaphores. Data moves between devices by JAX's collectives and lax.ppermute only.
A program may use at most 128 MiB of HBM per device.

v0:
```python
import jax
import jax.numpy as jnp
from jax import lax
from jax.sharding import Mesh
from jax.sharding import PartitionSpec as P

HDIM = 64
MP = ("mp_0", "mp_1")
DP = ("dp_0", "dp_1", "dp_2")
DP_MP = ("dp_0", "dp_1", "dp_2", "mp_0", "mp_1")


EPS = 1e-06


def shifted(block, axis, distance):
    devices = range(lax.axis_size(axis))
    route = [(i - distance, i) for i in devices if i - distance in devices]
    return lax.ppermute(block, axis, route)


def in_one_piece(arrays, axis, dim, along):
    widths = [a.shape[along] for a in arrays]
    both = jnp.concatenate(arrays, axis=along)
    result = lax.all_gather(both, axis, axis=dim, tiled=True)
    return tuple(jnp.split(result, [sum(widths[:k]) for k in range(1, len(widths))], axis=along))


def split_up(value, dim, devices):
    before, after = (value.shape[:dim], value.shape[dim + 1 :])
    return jnp.moveaxis(value.reshape(*before, devices, -1, *after), dim, 0)


def sum_packed(arrays, axis, dims):
    devices = lax.axis_size(axis)
    pieces = [split_up(a, dim, devices) for a, dim in zip(arrays, dims)]
    lines = jnp.concatenate([b.reshape(devices, -1) for b in pieces], axis=1)
    rows = max(16, -(-lines.shape[1] // 1024) * 8)
    lines = jnp.pad(lines, ((0, 0), (0, rows * 128 - lines.shape[1]))).reshape(-1, 128)
    ravelled, at, outs = (lax.psum_scatter(lines, axis, tiled=True).reshape(-1), 0, [])
    for b in pieces:
        part = b[0]
        outs.append(ravelled[at : at + part.size].reshape(part.shape))
        at += part.size
    return tuple(outs)


def with_halo(block, sides, width):
    for axis, dim in sides:
        count = lax.axis_size(axis)
        forward = [(i, i + 1) for i in range(count - 1)]
        backward = [(target, source) for source, target in forward]
        low = lax.ppermute(
            lax.slice_in_dim(block, block.shape[dim] - width, None, axis=dim), axis, forward
        )
        high = lax.ppermute(lax.slice_in_dim(block, 0, width, axis=dim), axis, backward)
        block = jnp.concatenate([low, block, high], axis=dim)
    return block


def over_axes(value, axes):
    for axis in axes:
        value = lax.psum(value, axis)
    return value


def sent_together(arrays, axis, dim, along):
    widths = [a.shape[along] for a in arrays]
    both = jnp.concatenate(arrays, axis=along)
    result = lax.psum_scatter(both, axis, scatter_dimension=dim, tiled=True)
    return tuple(jnp.split(result, [sum(widths[:k]) for k in range(1, len(widths))], axis=along))


def sent_and_summed(value, axis, dim):
    devices = lax.axis_size(axis)
    pieces = lax.all_to_all(split_up(value, dim, devices), axis, 0, 0, tiled=True)
    return jnp.sum(pieces.astype(jnp.float32), axis=0)


def sent_together_2(arrays, axis, dim, along):
    widths = [a.shape[along] for a in arrays]
    both = jnp.concatenate(arrays, axis=along)
    result = sent_and_summed(both, axis, dim)
    return tuple(jnp.split(result, [sum(widths[:k]) for k in range(1, len(widths))], axis=along))


def shards(
    grid_latent,
    mesh_latent,
    edge_source,
    edge_dest,
    edge_count,
    edge_attr,
    w_attr,
    w_in,
    w_out,
    w_qkv,
    w_o,
    cotangent,
):
    band = lax.axis_index(MP)
    grid_rows = grid_latent.shape[1]
    nodes = mesh_latent.shape[1]
    edges = edge_source.shape[1]
    grid = grid_latent[0]
    live = (jnp.arange(edges, dtype=jnp.int32) < edge_count[0, 0]).astype(jnp.float32)[:, None]
    source_local = edge_source[0] - band * grid_rows
    dest_local = edge_dest[0] - (band - 1) * nodes
    projected = jnp.dot(grid, w_in, preferred_element_type=jnp.float32)
    attr_terms = lax.dot_general(
        edge_attr[0],
        w_attr,
        (((0,), (0,)), ((), ())),
        precision=lax.Precision.HIGHEST,
        preferred_element_type=jnp.float32,
    )
    preact = projected[source_local] + attr_terms
    hidden = (jax.nn.silu(preact) * live).astype(jnp.bfloat16)
    message = jnp.dot(hidden, w_out, preferred_element_type=jnp.float32).astype(jnp.bfloat16)
    dest_table = (dest_local[:, None] == jnp.arange(3 * nodes, dtype=jnp.int32)[None, :]).astype(
        jnp.bfloat16
    )
    partial_rows = lax.dot_general(
        dest_table, message, (((0,), (0,)), ((), ())), preferred_element_type=jnp.float32
    )
    from_below = shifted(partial_rows[2 * nodes :], MP, 1)
    from_above = shifted(partial_rows[:nodes], MP, -1)
    node = (
        mesh_latent[0].astype(jnp.float32)
        + partial_rows[nodes : 2 * nodes]
        + from_below
        + from_above
    )
    inv = lax.rsqrt(jnp.mean(node * node, axis=-1, keepdims=True) + EPS)
    normed = (node * inv).astype(jnp.bfloat16)
    all_normed, all_cot = in_one_piece((normed, cotangent[0]), MP, 0, 1)
    total = all_normed.shape[0]
    width = w_qkv.shape[2]
    local_heads = width // HDIM
    qkv = jnp.einsum("nc,icd->ind", all_normed, w_qkv, preferred_element_type=jnp.float32).astype(
        jnp.bfloat16
    )
    qkv = qkv.reshape(3, total, local_heads, HDIM)
    query, keys, values = (qkv[0], qkv[1], qkv[2])
    d_att = lax.dot_general(
        all_cot, w_o, (((1,), (1,)), ((), ())), preferred_element_type=jnp.float32
    ).astype(jnp.bfloat16)
    d_att = d_att.reshape(total, local_heads, HDIM)
    block = min(512, total)
    scale = HDIM ** (-0.5)

    def attend_block(carry, index):
        key_acc, value_acc = carry
        start = index * block
        query_blk = lax.dynamic_slice_in_dim(query, start, block, 0)
        grad_blk = lax.dynamic_slice_in_dim(d_att, start, block, 0)
        scores = (
            jnp.einsum("qhd,khd->hqk", query_blk, keys, preferred_element_type=jnp.float32) * scale
        )
        probs = jax.nn.softmax(scores, axis=-1)
        probs_b = probs.astype(jnp.bfloat16)
        attended = jnp.einsum(
            "hqk,khd->qhd", probs_b, values, preferred_element_type=jnp.float32
        ).astype(jnp.bfloat16)
        dprob = jnp.einsum("qhd,khd->hqk", grad_blk, values, preferred_element_type=jnp.float32)
        delta = jnp.sum(probs * dprob, axis=-1, keepdims=True)
        dscore = (probs * (dprob - delta) * scale).astype(jnp.bfloat16)
        dquery = jnp.einsum(
            "hqk,khd->qhd", dscore, keys, preferred_element_type=jnp.float32
        ).astype(jnp.bfloat16)
        key_acc = key_acc + jnp.einsum(
            "hqk,qhd->khd", dscore, query_blk, preferred_element_type=jnp.float32
        )
        value_acc = value_acc + jnp.einsum(
            "hqk,qhd->khd", probs_b, grad_blk, preferred_element_type=jnp.float32
        )
        return ((key_acc, value_acc), (attended, dquery))

    empty = jnp.zeros((total, local_heads, HDIM), jnp.float32)
    sums, blocks = lax.scan(
        attend_block, (empty, empty), jnp.arange(total // block, dtype=jnp.int32)
    )
    attended = blocks[0].reshape(total, width)
    dquery = blocks[1].reshape(total, width)
    dkeys = sums[0].astype(jnp.bfloat16).reshape(total, width)
    dvalues = sums[1].astype(jnp.bfloat16).reshape(total, width)
    dqkv = jnp.stack([dquery, dkeys, dvalues])
    dw_o = lax.dot_general(
        attended, all_cot, (((0,), (0,)), ((), ())), preferred_element_type=jnp.float32
    )
    dw_qkv = jnp.einsum("nc,ind->icd", all_normed, dqkv, preferred_element_type=jnp.float32)
    sum_qkv, sum_o = tuple(
        (
            part.astype(jnp.float32)
            for part in sum_packed(
                (dw_qkv.astype(jnp.bfloat16), dw_o.astype(jnp.bfloat16)), DP, (1, 1)
            )
        )
    )
    dx = lax.psum_scatter(
        jnp.einsum("ind,icd->nc", dqkv, w_qkv, preferred_element_type=jnp.float32).astype(
            jnp.bfloat16
        ),
        MP,
        scatter_dimension=0,
        tiled=True,
    ).astype(jnp.float32)
    dnode = (
        cotangent[0].astype(jnp.float32)
        + inv * dx
        - node * inv * inv * inv * jnp.mean(dx * node, axis=-1, keepdims=True)
    )
    d_mesh = dnode.astype(jnp.bfloat16)
    beside_all = with_halo(d_mesh, ((MP, 0),), nodes)
    dmessage = (beside_all[dest_local].astype(jnp.float32) * live).astype(jnp.bfloat16)
    dw_out = lax.dot_general(
        hidden, dmessage, (((0,), (0,)), ((), ())), preferred_element_type=jnp.float32
    )
    dhidden = lax.dot_general(
        dmessage, w_out, (((1,), (1,)), ((), ())), preferred_element_type=jnp.float32
    )
    sigma = jax.nn.sigmoid(preact)
    dpre = dhidden * sigma * (1.0 + preact * (1.0 - sigma)) * live
    dw_attr = jnp.dot(
        edge_attr[0], dpre, precision=lax.Precision.HIGHEST, preferred_element_type=jnp.float32
    )
    source_table = (
        source_local[:, None] == jnp.arange(grid_rows, dtype=jnp.int32)[None, :]
    ).astype(jnp.bfloat16)
    dproj = lax.dot_general(
        source_table,
        dpre.astype(jnp.bfloat16),
        (((0,), (0,)), ((), ())),
        preferred_element_type=jnp.float32,
    ).astype(jnp.bfloat16)
    dw_in = lax.dot_general(
        grid, dproj, (((0,), (0,)), ((), ())), preferred_element_type=jnp.float32
    )
    d_grid = lax.dot_general(
        dproj, w_in, (((1,), (1,)), ((), ())), preferred_element_type=jnp.float32
    ).astype(jnp.bfloat16)
    sum_attr = over_axes(dw_attr, DP_MP)
    first_in, first_out = tuple(
        (
            part.astype(jnp.float32)
            for part in sent_together(
                (dw_in.astype(jnp.bfloat16), dw_out.astype(jnp.bfloat16)), MP, 1, 0
            )
        )
    )
    sum_in, sum_out = sent_together_2(
        (first_in.astype(jnp.bfloat16), first_out.astype(jnp.bfloat16)), DP, 0, 1
    )
    return (d_grid[None], d_mesh[None], sum_attr, sum_in, sum_out, sum_qkv, sum_o)


def solution(mesh):
    finer = Mesh(mesh.devices.reshape(2, 4, 2, 2, 8), ("dp_0", "dp_1", "dp_2", "mp_0", "mp_1"))
    in_specs = (
        P(DP, MP, None),
        P(DP, MP, None),
        P(DP, MP),
        P(DP, MP),
        P(DP, MP),
        P(DP, None, MP),
        P(),
        P(),
        P(),
        P(None, None, MP),
        P(MP, None),
        P(DP, MP, None),
    )
    out_specs = (
        P(DP, MP, None),
        P(DP, MP, None),
        P(),
        P(DP, MP),
        P(DP, MP),
        P(None, DP, MP),
        P(MP, DP),
    )
    return jax.shard_map(
        shards, mesh=finer, in_specs=in_specs, out_specs=out_specs, check_vma=False
    )
```

profile of v0, /device:TPU:1, one launch (start us, length us, event | category | flops | bytes accessed | tf_op | source)
XLA Modules:
  0.0 509.2 jit_solution(17701429254281925764)
XLA Ops:
  11.3 3.7 gather_fusion
  15.0 5.5 %convolution_add_fusion = f32[768,1024]{1,0:T(8,128)} fusion(f32[768,1024]{1,0:T(8,128)} %gather_fusion, f32[4,1024]{1,0:T(4,128)S(1)} %copy-done.18, f32[1,4,768]{2,1,0:T(4,128)S(1)} %copy-done.17), kind=kOutput, calls=%fused_computation.56 | convolution fusion | flops 38535168 | bytes 6320128 | tf_op jit(solution)/shard_map/dot_general | solution.py:110
  20.5 5.6 %fusion.55 = f32[384,1024]{1,0:T(8,128)} fusion(bf16[1024,1024]{1,0:T(8,128)(2,1)S(1)} %copy-done, s32[768]{0:T(1024)S(1)} %subtract_reduce_fusion, f32[768,1024]{1,0:T(8,128)} %convolution_add_fusion, f32[768]{0:T(1024)S(1)} %fusion.72), kind=kOutput, calls=%fused_computation.67 | convolution fusion | flops 2220392448 | bytes 6821888 | tf_op jit(solution)/shard_map/dot_general | solution.py:123
  27.4 4.4 collective-permute-start
  33.1 9.3 %collective-permute-done = f32[128,1024]{1,0:T(8,128)S(1)} collective-permute-done((f32[128,1024]{1,0:T(8,128)S(1)}, f32[128,1024]{1,0:T(8,128)S(1)}, u32[]{:S(2)}, u32[]{:S(2)}) %collective-permute-start) | collective-permute-done | bytes 524320 | tf_op jit(solution)/shard_map/ppermute | solution.py:19
  42.4 4.2 collective-permute-done.1
  49.9 104.3 %all-gather.2.cloned.1.call-done = bf16[2048,2048]{1,0:T(8,128)(2,1)} async-done(((bf16[128,2048]{1,0:T(8,128)(2,1)}), bf16[2048,2048]{1,0:T(8,128)(2,1)}) %all-gather.2.cloned.1.call-update) | async-done | bytes 8388624 | tf_op jit(solution)/shard_map/all_gather | solution.py:25
  154.1 3.9 fusion.35
  161.2 71.8 %while.17 = (s32[]{:T(128)}, f32[2048,1,64]{0,2,1:T(8,128)S(1)}, f32[2048,1,64]{0,2,1:T(8,128)S(1)}, bf16[4,512,1,64]{1,3,2,0:T(8,128)(2,1)}, bf16[4,512,1,64]{1...) while((s32[]{:T(128)}, f32[2048,1,64]{0,2,1:T(8,128)S(1)}, ...), condition=%wide.region_5.6_spmd.clone, body=%wide.region_1.5_spmd.clone.sunk | while | flops 822671872 | bytes 83246416 | solution.py:180
  235.9 4.3 bitcast_convert_fusion
  253.2 55.9 %reduce-scatter.6.cloned.1.call-done = bf16[128,1024]{1,0:T(8,128)(2,1)} async-done(((bf16[2048,1024]{1,0:T(8,128)(2,1)}), bf16[128,1024]{1,0:T(8,128)(2,1)}) %reduce-scatter.6.cloned.1.call-update) | async-done | bytes 262160 | tf_op jit(solution)/shard_map/reduce_scatter | solution.py:200
  317.1 3.5 collective-permute-done.3
  321.8 3.6 gather_fusion.1
  325.4 4.7 convolution_convert_fusion.2
  338.6 6.5 %copy.32 = bf16[2048,1024]{0,1:T(8,128)(2,1)} copy(bf16[2048,1024]{1,0:T(8,128)(2,1)} %pad_maximum_fusion) | data formatting | bytes 8388608
  345.1 53.2 %reduce-scatter.8.cloned.1.call-done = bf16[128,128]{1,0:T(8,128)(2,1)} async-done(((bf16[2048,128]{1,0:T(8,128)(2,1)}), bf16[128,128]{1,0:T(8,128)(2,1)}) %reduce-scatter.8.cloned.1.call-update) | async-done | bytes 32784 | tf_op jit(solution)/shard_map/reduce_scatter | solution.py:40
  401.2 3.6 convolution_bitcast_fusion.2
  404.8 8.2 %psum.35 = f32[4,1024]{1,0:T(4,128)S(1)} all-reduce(f32[4,1024]{1,0:T(4,128)S(1)} %convolution_bitcast_fusion.2), channel_id=1, replica_groups=mesh['dp_0'=2,'dp_1'=4,'dp_2'=2,'mp_0'=2,'mp_1'=8] {'dp_0'}, use_global_device_ids=true, to_apply=%region_8.9 | all-reduce | flops 4096 | bytes 32768 | tf_op jit(solution)/shard_map/psum | solution.py:63
  413.0 12.0 %psum.36 = f32[4,1024]{1,0:T(4,128)S(1)} all-reduce(f32[4,1024]{1,0:T(4,128)S(1)} %psum.35), channel_id=1, replica_groups=mesh['dp_0'=2,'dp_1'=4,'dp_2'=2,'mp_0'=2,'mp_1'=8] {'dp_1'}, use_global_device_ids=true, to_apply=%region_9.10 | all-reduce | flops 4096 | bytes 32768 | tf_op jit(solution)/shard_map/psum | solution.py:63
  425.0 11.2 %psum.37 = f32[4,1024]{1,0:T(4,128)S(1)} all-reduce(f32[4,1024]{1,0:T(4,128)S(1)} %psum.36), channel_id=1, replica_groups=mesh['dp_0'=2,'dp_1'=4,'dp_2'=2,'mp_0'=2,'mp_1'=8] {'dp_2'}, use_global_device_ids=true, to_apply=%region_10.11 | all-reduce | flops 4096 | bytes 32768 | tf_op jit(solution)/shard_map/psum | solution.py:63
  436.2 8.4 %psum.38 = f32[4,1024]{1,0:T(4,128)S(1)} all-reduce(f32[4,1024]{1,0:T(4,128)S(1)} %psum.37), channel_id=1, replica_groups=mesh['dp_0'=2,'dp_1'=4,'dp_2'=2,'mp_0'=2,'mp_1'=8] {'mp_0'}, use_global_device_ids=true, to_apply=%region_11.12 | all-reduce | flops 4096 | bytes 32768 | tf_op jit(solution)/shard_map/psum | solution.py:63
  444.6 26.3 %psum.39 = f32[4,1024]{1,0:T(4,128)} all-reduce(f32[4,1024]{1,0:T(4,128)S(1)} %psum.38), channel_id=1, replica_groups=mesh['dp_0'=2,'dp_1'=4,'dp_2'=2,'mp_0'=2,'mp_1'=8] {'mp_1'}, use_global_device_ids=true, to_apply=%region_12.13 | all-reduce | flops 4096 | bytes 32768 | tf_op jit(solution)/shard_map/psum | solution.py:63
  474.7 18.5 %all-to-all-start = ((bf16[16,64,128]{2,1,0:T(8,128)(2,1)}), bf16[16,64,128]{2,1,0:T(8,128)(2,1)S(1)}, u32[]{:S(2)}, u32[]{:S(2)}) async-start(bf16[16,64,128]{2,1,0:T(8,128)(2,1)} %bitcast.22), calls=%async_computation.1 | async-start | bytes 524288 | tf_op jit(solution)/shard_map/all_to_all | solution.py:76
  496.4 5.6 %all-to-all-done = bf16[16,64,128]{2,1,0:T(8,128)(2,1)S(1)} async-done(((bf16[16,64,128]{2,1,0:T(8,128)(2,1)}), bf16[16,64,128]{2,1,0:T(8,128)(2,1)S(1)}, u32[]{:S(2)}, u32[]{:S(2)}) %all-to-all-start) | async-done | bytes 262176 | tf_op jit(solution)/shard_map/all_to_all | solution.py:76
  (184 shorter events, 125.3 us)
Async XLA Ops:
  7.2 13.3 %copy-start = (bf16[1024,1024]{1,0:T(8,128)(2,1)S(1)}, bf16[1024,1024]{1,0:T(8,128)(2,1)}, u32[]{:S(2)}) copy-start(bf16[1024,1024]{1,0:T(8,128)(2,1)} %param.22) | copy-start | bytes 6291460
  7.2 147.0 %all-gather.2.cloned.1.call-start = ((), (), s32[]{:S(2)}) async-start(), calls=%async_computation.4 | async-start | bytes 8912896 | tf_op jit(solution)/shard_map/all_gather | solution.py:25
  8.7 11.7 %copy-start.22 = (f32[768]{0:T(1024)}, f32[768]{0:T(1024)S(1)}, u32[]{:S(2)}) copy-start(f32[768]{0:T(1024)S(1)} %fusion.72) | copy-start | bytes 9220
  20.5 26.1 %copy-start.13 = (bf16[1,128,1024]{2,1,0:T(8,128)(2,1)S(1)}, bf16[1,128,1024]{2,1,0:T(8,128)(2,1)}, u32[]{:S(2)}) copy-start(bf16[1,128,1024]{2,1,0:T(8,128)(2,1)} %param.15) | copy-start | bytes 786436
  26.1 22.7 %copy-start.11 = (bf16[1,128,1024]{2,1,0:T(8,128)(2,1)S(1)}, bf16[1,128,1024]{2,1,0:T(8,128)(2,1)}, u32[]{:S(2)}) copy-start(bf16[1,128,1024]{2,1,0:T(8,128)(2,1)} %param.25) | copy-start | bytes 786436
  26.1 128.1 %copy-start.26 = (bf16[3,1024,64]{1,2,0:T(8,128)(2,1)S(1)}, bf16[3,1024,64]{1,2,0:T(8,128)(2,1)}, u32[]{:S(2)}) copy-start(bf16[3,1024,64]{1,2,0:T(8,128)(2,1)} %param.23) | copy-start | bytes 1179652
  27.4 15.0 %collective-permute-start = (f32[128,1024]{1,0:T(8,128)S(1)}, f32[128,1024]{1,0:T(8,128)S(1)}, u32[]{:S(2)}, u32[]{:S(2)}) collective-permute-start(f32[128,1024]{1,0:T(8,128)S(1)} %get-tuple-element.136), channel_id=1, source_target_pairs={{0,1},{1,2},{2,3},{3,4},{4,5},{5,6},{6,7},{7,8},{8,9},{9,10},{10,1... | collective-permute-start | bytes 1572872 | tf_op jit(solution)/shard_map/ppermute | solution.py:19
  31.8 14.7 %collective-permute-start.1 = (f32[128,1024]{1,0:T(8,128)S(1)}, f32[128,1024]{1,0:T(8,128)S(1)}, u32[]{:S(2)}, u32[]{:S(2)}) collective-permute-start(f32[128,1024]{1,0:T(8,128)S(1)} %get-tuple-element.137), channel_id=1, source_target_pairs={{1,0},{2,1},{3,2},{4,3},{5,4},{6,5},{7,6},{8,7},{9,8},{10,9},{11,1... | collective-permute-start | bytes 1572872 | tf_op jit(solution)/shard_map/ppermute | solution.py:19
  49.6 259.5 %reduce-scatter.6.cloned.1.call-start = ((), (), s32[]{:S(2)}) async-start(), calls=%async_computation.5 | async-start | bytes 4456448 | tf_op jit(solution)/shard_map/reduce_scatter | solution.py:200
  154.1 4.8 copy-start.25
  171.0 5.3 %copy-start.2 = (f32[512,2048]{1,0:T(8,128)S(1)}, f32[512,2048]{1,0:T(8,128)}, u32[]{:S(2)}) copy-start(f32[512,2048]{1,0:T(8,128)} %copy-done.1) | copy-start | bytes 12582916 | tf_op jit(solution)/shard_map/while
  189.0 5.3 %copy-start.2 = (f32[512,2048]{1,0:T(8,128)S(1)}, f32[512,2048]{1,0:T(8,128)}, u32[]{:S(2)}) copy-start(f32[512,2048]{1,0:T(8,128)} %copy-done.1) | copy-start | bytes 12582916 | tf_op jit(solution)/shard_map/while
  206.9 5.3 %copy-start.2 = (f32[512,2048]{1,0:T(8,128)S(1)}, f32[512,2048]{1,0:T(8,128)}, u32[]{:S(2)}) copy-start(f32[512,2048]{1,0:T(8,128)} %copy-done.1) | copy-start | bytes 12582916 | tf_op jit(solution)/shard_map/while
  224.9 5.3 %copy-start.2 = (f32[512,2048]{1,0:T(8,128)S(1)}, f32[512,2048]{1,0:T(8,128)}, u32[]{:S(2)}) copy-start(f32[512,2048]{1,0:T(8,128)} %copy-done.1) | copy-start | bytes 12582916 | tf_op jit(solution)/shard_map/while
  240.2 158.1 %reduce-scatter.8.cloned.1.call-start = ((), (), s32[]{:S(2)}) async-start(), calls=%async_computation.6 | async-start | bytes 557056 | tf_op jit(solution)/shard_map/reduce_scatter | solution.py:40
  249.6 59.5 %copy-start.7 = (f32[128,1024]{1,0:T(8,128)S(1)}, f32[128,1024]{1,0:T(8,128)}, u32[]{:S(2)}) copy-start(f32[128,1024]{1,0:T(8,128)} %copy-done.6) | copy-start | bytes 1572868
  253.2 68.5 %copy-start.19 = (s32[1024]{0:T(1024)S(1)}, s32[1024]{0:T(1024)}, u32[]{:S(2)}) copy-start(s32[1024]{0:T(1024)} %pad_clamp_fusion) | copy-start | bytes 12292
  311.5 13.9 %copy-start.12 = (bf16[128,1024]{1,0:T(8,128)(2,1)}, bf16[128,1024]{1,0:T(8,128)(2,1)S(1)}, u32[]{:S(2)}) copy-start(bf16[128,1024]{1,0:T(8,128)(2,1)S(1)} %fusion.62) | copy-start | bytes 786436
  311.5 5.7 %collective-permute-start.2 = (bf16[128,1024]{1,0:T(8,128)(2,1)S(1)}, bf16[128,1024]{1,0:T(8,128)(2,1)}, u32[]{:S(2)}, u32[]{:S(2)}) collective-permute-start(bf16[128,1024]{1,0:T(8,128)(2,1)S(1)} %fusion.62), channel_id=1, source_target_pairs={{0,1},{1,2},{2,3},{3,4},{4,5},{5,6},{6,7},{7,8},{8,9},{9,10},{10,1... | collective-permute-start | bytes 786440 | tf_op jit(solution)/shard_map/ppermute | solution.py:53
  313.5 7.2 %collective-permute-start.3 = (bf16[128,1024]{1,0:T(8,128)(2,1)S(1)}, bf16[128,1024]{1,0:T(8,128)(2,1)}, u32[]{:S(2)}, u32[]{:S(2)}) collective-permute-start(bf16[128,1024]{1,0:T(8,128)(2,1)S(1)} %fusion.62), channel_id=1, source_target_pairs={{1,0},{2,1},{3,2},{4,3},{5,4},{6,5},{7,6},{8,7},{9,8},{10,9},{11,1... | collective-permute-start | bytes 786440 | tf_op jit(solution)/shard_map/ppermute | solution.py:56
  315.9 156.7 %reduce-scatter.10.cloned.1.call-start = ((), (), s32[]{:S(2)}) async-start(), calls=%async_computation.7 | async-start | bytes 4456448
  325.4 4.7 copy-start.8
  325.4 4.7 copy-start.10
  474.7 27.2 %all-to-all-start = ((bf16[16,64,128]{2,1,0:T(8,128)(2,1)}), bf16[16,64,128]{2,1,0:T(8,128)(2,1)S(1)}, u32[]{:S(2)}, u32[]{:S(2)}) async-start(bf16[16,64,128]{2,1,0:T(8,128)(2,1)} %bitcast.22), calls=%async_computation.1 | async-start | bytes 524288 | tf_op jit(solution)/shard_map/all_to_all | solution.py:76
  (25 other events, 41.5 us)
Sparse Core Ops, SparseCore 0:
  49.7 104.3 all-gather.1
  240.4 68.7 reduce-scatter.5
  316.0 82.3 reduce-scatter.7
  400.8 71.7 reduce-scatter.9
where the time goes:
time: 511 us; the launch traced here: 509 us
  waiting for transfers between devices  239 us (47%)
  matrix products  93.3 us (18%)
  blocking collectives  66.1 us (13%)
  local copies, waits for them, and re-layouts  42.6 us (8%)
  starting transfers between devices  28 us (5%)
  other arithmetic  22.7 us (4%)
  between operations  14.9 us (3%)
    all_gather x1, waiting for transfers between devices, in_one_piece(): result = lax.all_gather(both, axis, axis=dim, tiled=True)  104 us
    psum x5, blocking collectives, over_axes(): value = lax.psum(value, axis)  66.1 us
    reduce_scatter x1, waiting for transfers between devices, shards(): lax.psum_scatter(jnp.einsum('ind,icd->nc', dqkv, w_qkv, preferred_element...  55.9 us
    reduce_scatter x1, waiting for transfers between devices, sum_packed(): lax.psum_scatter(lines, axis, tiled=True).reshape(-1)  53.2 us
    all_to_all x1, starting transfers between devices, sent_and_summed(): lax.all_to_all(split_up(value, dim, devices), axis, 0, 0, tiled=True)  18.5 us
    ppermute x2, waiting for transfers between devices, shifted(): return lax.ppermute(block, axis, route)  13.4 us
    dot_general x4, matrix products, attend_block(): jnp.einsum('hqk,khd->qhd', dscore, keys, preferred_element_type=jnp.float32)  11.9 us
    unnamed x52, local copies, waits for them, and re-layouts  10.7 us
  transfers between devices with their start and end apart: 9, of which 9 were waited for; matrix products, arithmetic and copies ran while one was open for 9% of the time, Pallas kernels for 0%

commit v1 on v0

v1 whole, which is shorter than its diff:
```python
import functools

import jax
import jax.numpy as jnp
from jax import lax
from jax.experimental import pallas as pl
from jax.experimental.pallas import tpu as pltpu
from jax.sharding import Mesh
from jax.sharding import PartitionSpec as P

HDIM = 64
SCALE = HDIM ** (-0.5)
MP = ("mp_0", "mp_1")
DP = ("dp_0", "dp_1", "dp_2")
GROUP = ("dp_0", "dp_1")
CORE = "dp_2"
EPS = 1e-06
BF = jnp.bfloat16
F32 = jnp.float32
NN = (((1,), (0,)), ((), ()))
NT = (((1,), (1,)), ((), ()))
TN = (((0,), (0,)), ((), ()))


def dot(a, b, dims):
    return lax.dot_general(a, b, dims, preferred_element_type=F32)


def shifted(block, axis, distance):
    devices = range(lax.axis_size(axis))
    route = [(i - distance, i) for i in devices if i - distance in devices]
    return lax.ppermute(block, axis, route)


def swapped(block):
    return lax.ppermute(block, CORE, [(0, 1), (1, 0)])


def after(value, earlier):
    return lax.optimization_barrier((value, earlier))[0]


def both_halves(mine, other, core):
    low = jnp.where(core == 0, mine, other)
    high = jnp.where(core == 0, other, mine)
    return jnp.concatenate([low, high], axis=1)


def column_half(value, half):
    width = value.shape[1] // 2
    return lax.dynamic_slice_in_dim(value, half * width, width, 1)


def attend_kernel(qkv_ref, da_ref, out_ref, k_s, v_s, kt_s, vt_s, dk_s, dv_s, *, block, steps):
    i = pl.program_id(0)

    @pl.when(i == 0)
    def _():
        k = qkv_ref[:, HDIM : 2 * HDIM]
        v = qkv_ref[:, 2 * HDIM : 3 * HDIM]
        k_s[...] = k
        v_s[...] = v
        kt_s[...] = k.T
        vt_s[...] = v.T
        dk_s[...] = jnp.zeros_like(dk_s)
        dv_s[...] = jnp.zeros_like(dv_s)

    rows = pl.ds(pl.multiple_of(i * block, block), block)
    q = qkv_ref[rows, 0:HDIM] * jnp.asarray(SCALE, BF)
    da = da_ref[rows, :]
    s = dot(k_s[...], q, NT)
    dp = dot(v_s[...], da, NT)
    e = jnp.exp(s - jnp.max(s, axis=0, keepdims=True))
    p = e * (1.0 / jnp.sum(e, axis=0, keepdims=True))
    delta = jnp.sum(p * dp, axis=0, keepdims=True)
    pb = p.astype(BF)
    ds = (p * (dp - delta)).astype(BF)
    out_ref[3 * HDIM : 4 * HDIM, rows] = dot(vt_s[...], pb, NN).astype(BF)
    out_ref[0:HDIM, rows] = (dot(kt_s[...], ds, NN) * SCALE).astype(BF)
    dk_s[...] += dot(ds, q, NN)
    dv_s[...] += dot(pb, da, NN)

    @pl.when(i == steps - 1)
    def _():
        out_ref[HDIM : 2 * HDIM, :] = dk_s[...].T.astype(BF)
        out_ref[2 * HDIM : 3 * HDIM, :] = dv_s[...].T.astype(BF)


def attend(qkv, da):
    total = qkv.shape[0]
    block = min(512, total)
    steps = total // block
    return pl.pallas_call(
        functools.partial(attend_kernel, block=block, steps=steps),
        grid=(steps,),
        in_specs=[
            pl.BlockSpec((total, 3 * HDIM), lambda i: (0, 0)),
            pl.BlockSpec((total, HDIM), lambda i: (0, 0)),
        ],
        out_specs=pl.BlockSpec((4 * HDIM, total), lambda i: (0, 0)),
        out_shape=jax.ShapeDtypeStruct((4 * HDIM, total), BF),
        scratch_shapes=[
            pltpu.VMEM((total, HDIM), BF),
            pltpu.VMEM((total, HDIM), BF),
            pltpu.VMEM((HDIM, total), BF),
            pltpu.VMEM((HDIM, total), BF),
            pltpu.VMEM((total, HDIM), F32),
            pltpu.VMEM((total, HDIM), F32),
        ],
        compiler_params=pltpu.CompilerParams(dimension_semantics=("arbitrary",)),
        cost_estimate=pl.CostEstimate(
            flops=24 * total * total * HDIM,
            transcendentals=total * total,
            bytes_accessed=20 * total * HDIM,
        ),
        name="attend",
    )(qkv, da)


def shards(
    grid_latent,
    mesh_latent,
    edge_source,
    edge_dest,
    edge_count,
    edge_attr,
    w_attr,
    w_in,
    w_out,
    w_qkv,
    w_o,
    cotangent,
):
    band = lax.axis_index(MP)
    core = lax.axis_index(CORE)
    bands = lax.axis_size(MP)
    groups = lax.axis_size(GROUP)
    grid_rows = grid_latent.shape[1]
    nodes = mesh_latent.shape[1]
    edges = edge_source.shape[1]
    channels = grid_latent.shape[2]
    grid = grid_latent[0]
    cot = cotangent[0]
    live = (jnp.arange(edges, dtype=jnp.int32) < edge_count[0, 0]).astype(F32)[:, None]
    source_local = edge_source[0] - band * grid_rows
    dest_local = edge_dest[0] - (band - 1) * nodes

    o_mine = lax.all_gather(column_half(w_o, core), MP, axis=0, tiled=True)
    o_other = swapped(o_mine)

    projected = dot(grid, w_in, NN)
    attr_columns = edge_attr[0].T
    attr_terms = sum(
        attr_columns[:, a : a + 1] * w_attr[a : a + 1] for a in range(w_attr.shape[0])
    )
    preact = projected[source_local] + attr_terms
    hidden = (jax.nn.silu(preact) * live).astype(BF)
    message = dot(hidden, w_out, NN).astype(BF)
    dest_table = (dest_local[:, None] == jnp.arange(3 * nodes, dtype=jnp.int32)[None, :]).astype(BF)
    partial_rows = dot(dest_table, message, TN)
    from_below = shifted(partial_rows[2 * nodes :].astype(BF), MP, 1)
    from_above = shifted(partial_rows[:nodes].astype(BF), MP, -1)
    node = (
        mesh_latent[0].astype(F32)
        + partial_rows[nodes : 2 * nodes]
        + from_below.astype(F32)
        + from_above.astype(F32)
    )
    inv = lax.rsqrt(jnp.mean(node * node, axis=-1, keepdims=True) + EPS)
    normed = (node * inv).astype(BF)
    all_normed = lax.all_gather(normed, MP, axis=0, tiled=True)

    d_att = (
        dot(column_half(cot, core), o_mine, NT) + dot(column_half(cot, 1 - core), o_other, NT)
    ).astype(BF)
    width = w_qkv.shape[2]
    d_att = d_att.reshape(2, nodes // 2, bands, width).transpose(2, 1, 0, 3)
    d_att = d_att.reshape(bands, nodes // 2, 2 * width)
    d_att = lax.all_to_all(d_att, MP, 0, 0, tiled=True)
    d_att = d_att.reshape(bands, nodes // 2, 2, width).transpose(0, 2, 1, 3)
    d_att = d_att.reshape(bands * nodes, width)

    w_rows = jnp.concatenate([w_qkv[0], w_qkv[1], w_qkv[2]], axis=1)
    qkv = dot(all_normed, w_rows, NN).astype(BF)
    result = attend(qkv, d_att)
    dqkv = result[: 3 * width]

    w_heads = w_qkv.transpose(0, 2, 1).reshape(3 * width, channels)
    w_half = after(column_half(w_heads, core), all_normed)
    w_mine = lax.all_gather(w_half, MP, axis=0, tiled=True)
    w_other = swapped(w_mine)
    pieces = dqkv.reshape(3 * width, bands, nodes).transpose(1, 0, 2)
    pieces = lax.all_to_all(pieces, MP, 0, 0, tiled=True)
    pieces = pieces.reshape(bands * 3 * width, nodes)
    dx = both_halves(dot(pieces, w_mine, TN), dot(pieces, w_other, TN), core)

    all_cot = lax.all_gather(after(cot, w_mine), MP, axis=0, tiled=True)

    dnode = (
        cot.astype(F32)
        + inv * dx
        - node * inv * inv * inv * jnp.mean(dx * node, axis=-1, keepdims=True)
    )
    d_mesh = dnode.astype(BF)
    low = shifted(d_mesh, MP, 1)
    high = shifted(d_mesh, MP, -1)
    beside_all = jnp.concatenate([low, d_mesh, high], axis=0)
    dmessage = (beside_all[dest_local].astype(F32) * live).astype(BF)
    dw_out = dot(hidden, dmessage, TN).astype(BF)
    dhidden = dot(dmessage, w_out, NT)
    sigma = jax.nn.sigmoid(preact)
    dpre = dhidden * sigma * (1.0 + preact * (1.0 - sigma)) * live
    dw_attr = jnp.dot(
        edge_attr[0], dpre, precision=lax.Precision.HIGHEST, preferred_element_type=F32
    )
    source_table = (
        source_local[:, None] == jnp.arange(grid_rows, dtype=jnp.int32)[None, :]
    ).astype(BF)
    dproj = dot(source_table, dpre.astype(BF), TN).astype(BF)
    dw_in = dot(grid, dproj, TN).astype(BF)
    d_grid = dot(dproj, w_in, NT).astype(BF)

    dw_x = dot(all_normed, dqkv, (((0,), (1,)), ((), ())))
    dw_c = dot(all_cot, result[3 * width :], (((0,), (1,)), ((), ())))
    dw_heads = jnp.concatenate([dw_x, dw_c], axis=1).astype(BF)
    dw_heads = dw_heads.reshape(2 * groups, -1, 4 * width)
    dw_heads = lax.all_to_all(dw_heads, DP, 0, 0, tiled=True)
    sum_heads = jnp.sum(dw_heads.astype(F32), axis=0)
    sum_qkv = jnp.stack([sum_heads[:, j * width : (j + 1) * width] for j in range(3)])
    sum_o = sum_heads[:, 3 * width :].T

    rows = channels // (2 * groups)
    both = jnp.stack(
        [dw_in.reshape(groups, 2, rows, channels), dw_out.reshape(groups, 2, rows, channels)],
        axis=2,
    )
    mine = lax.dynamic_index_in_dim(both, core, 1, keepdims=False)
    theirs = lax.dynamic_index_in_dim(both, 1 - core, 1, keepdims=False)
    pair = mine.astype(F32) + swapped(theirs).astype(F32)
    pair = pair.astype(BF).reshape(groups, 2 * rows, channels)
    attr = dw_attr + swapped(dw_attr)
    attr_rows = attr.shape[0]
    attr_high = attr.astype(BF)
    attr_low = (attr - attr_high.astype(F32)).astype(BF)
    blank = jnp.zeros((16 - 2 * attr_rows, channels), BF)
    tail = jnp.concatenate([attr_high, attr_low, blank], axis=0)
    pair = jnp.concatenate([pair, jnp.broadcast_to(tail[None], (groups, 16, channels))], axis=1)
    pair = lax.all_to_all(pair, GROUP, 0, 0, tiled=True)
    summed = jnp.sum(pair.astype(F32), axis=0)
    attr = summed[2 * rows : 2 * rows + attr_rows]
    attr = attr + summed[2 * rows + attr_rows : 2 * rows + 2 * attr_rows]
    cols = channels // bands
    blocks = summed[: 2 * rows].astype(BF).reshape(2, rows, bands, cols)
    blocks = blocks.transpose(2, 1, 0, 3).reshape(bands, rows, 2 * cols)
    tail = attr.astype(BF).reshape(1, -1, 2 * cols)
    tail = jnp.broadcast_to(tail, (bands,) + tail.shape[1:])
    blocks = jnp.concatenate([blocks, tail], axis=1)
    blocks = lax.all_to_all(blocks, MP, 0, 0, tiled=True)
    summed = jnp.sum(blocks.astype(F32), axis=0)
    sum_in = summed[:rows, :cols]
    sum_out = summed[:rows, cols:]
    sum_attr = summed[rows:].reshape(attr.shape)
    return (d_grid[None], d_mesh[None], sum_attr, sum_in, sum_out, sum_qkv, sum_o)


def solution(mesh):
    finer = Mesh(mesh.devices.reshape(2, 4, 2, 2, 8), ("dp_0", "dp_1", "dp_2", "mp_0", "mp_1"))
    in_specs = (
        P(DP, MP, None),
        P(DP, MP, None),
        P(DP, MP),
        P(DP, MP),
        P(DP, MP),
        P(DP, None, MP),
        P(),
        P(),
        P(),
        P(None, None, MP),
        P(MP, None),
        P(DP, MP, None),
    )
    out_specs = (
        P(DP, MP, None),
        P(DP, MP, None),
        P(),
        P(DP, MP),
        P(DP, MP),
        P(None, DP, MP),
        P(MP, DP),
    )
    return jax.shard_map(
        shards, mesh=finer, in_specs=in_specs, out_specs=out_specs, check_vma=False
    )
```

time: 511 us -> 468 us (0.916)
  matrix products: 93.3 us -> 40 us
  starting transfers between devices: 28 us -> 54.8 us
  Pallas kernels: 0 us -> 20.8 us
  local copies, waits for them, and re-layouts: 42.6 us -> 28 us
  other arithmetic: 22.7 us -> 14.8 us
  waiting for transfers between devices: 239 us -> 233 us
  blocking collectives: 66.1 us -> 60.7 us
    reduce_scatter x2 -> x0, waiting for transfers between devices: 109 us -> none  [the longest x1 55.9 us: shards(): lax.psum_scatter(jnp.einsum('ind,icd->nc', dqkv, w_qkv, preferred_element...]
    all_gather x1 -> x4, waiting for transfers between devices: 104 us -> 189 us  [the longest x1 67.9 us: shards(): all_normed = lax.all_gather(normed, MP, axis=0, tiled=True)]
    psum x5 -> x0, blocking collectives: 66.1 us -> none  [over_axes(): value = lax.psum(value, axis)]
    all_to_all x0 -> x1, blocking collectives: none -> 60.7 us  [shards(): pair = lax.all_to_all(pair, GROUP, 0, 0, tiled=True)]
    dot_general x36 -> x14, matrix products: 85.9 us -> 38.2 us  [dot(): return lax.dot_general(a, b, dims, preferred_element_type=F32)]
    ppermute x2 -> x4, starting transfers between devices: 3.27 us -> 25.9 us  [swapped(): return lax.ppermute(block, CORE, [(0, 1), (1, 0)])]
    all_to_all x1 -> x4, waiting for transfers between devices: 5.57 us -> 27.5 us  [the longest x1 19.7 us: shards(): pieces = lax.all_to_all(pieces, MP, 0, 0, tiled=True)]
    pallas_call x0 -> x1, Pallas kernels: none -> 20.8 us  [attend(): pl.pallas_call(functools.partial(attend_kernel, block=block, steps=steps)...]
  transfers between devices with their start and end apart: 9 -> 16, of which waited for: 9 -> 12; matrix products, arithmetic and copies ran while one was open for 9% -> 12% of each run, Pallas kernels for 0% -> 4%
where the time goes in v1:
time: 468 us; the launch traced here: 467 us
  waiting for transfers between devices  233 us (50%)
  blocking collectives  60.7 us (13%)
  starting transfers between devices  54.8 us (12%)
  matrix products  40 us (9%)
  local copies, waits for them, and re-layouts  28 us (6%)
  Pallas kernels  20.8 us (4%)
  between operations  15.1 us (3%)
  other arithmetic  14.8 us (3%)
    all_gather x1, waiting for transfers between devices, shards(): all_normed = lax.all_gather(normed, MP, axis=0, tiled=True)  67.9 us
    all_gather x1, waiting for transfers between devices, shards(): o_mine = lax.all_gather(column_half(w_o, core), MP, axis=0, tiled=True)  67.5 us
    all_to_all x1, blocking collectives, shards(): pair = lax.all_to_all(pair, GROUP, 0, 0, tiled=True)  60.7 us
    all_gather x1, waiting for transfers between devices, shards(): w_mine = lax.all_gather(w_half, MP, axis=0, tiled=True)  54 us
    dot_general x14, matrix products, dot(): return lax.dot_general(a, b, dims, preferred_element_type=F32)  38.2 us
    ppermute x4, starting transfers between devices, swapped(): return lax.ppermute(block, CORE, [(0, 1), (1, 0)])  25.9 us
    pallas_call x1, Pallas kernels, attend(): pl.pallas_call(functools.partial(attend_kernel, block=block, steps=steps)...  20.8 us
    all_to_all x1, waiting for transfers between devices, shards(): pieces = lax.all_to_all(pieces, MP, 0, 0, tiled=True)  19.7 us
  transfers between devices with their start and end apart: 16, of which 12 were waited for; matrix products, arithmetic and copies ran while one was open for 12% of the time, Pallas kernels for 4%

profile of v1, /device:TPU:1, one launch (start us, length us, event | category | flops | bytes accessed | tf_op | source)
XLA Modules:
  0.0 467.0 jit_solution(11053978018985209481)
XLA Ops:
  13.1 3.7 gather_fusion
  17.4 4.1 multiply_convert_fusion.1
  21.6 5.3 %fusion.42 = (bf16[384,1024]{1,0:T(8,128)(2,1)}, f32[384,1024]{1,0:T(8,128)}) fusion(bf16[768,1024]{1,0:T(8,128)(2,1)} %multiply_convert_fusion.1, bf16[1024,1024]{1,0:T(8,128)(2,1)S(1)} %copy-done, s32[768]{0:T(1024)S(1)} %get-tuple-element.75), kind=kOutput, calls=%fused_computation.110 | convolution fusion | flops 2216067072 | bytes 6032384 | tf_op jit(solution)/shard_map/dot_general | solution.py:26
  28.1 4.4 collective-permute-start
  33.8 3.7 collective-permute-done
  37.4 4.2 collective-permute-done.1
  46.0 67.9 %all-gather.5.cloned.1.call-done = bf16[2048,1024]{1,0:T(8,128)(2,1)} async-done(((bf16[128,1024]{1,0:T(8,128)(2,1)}), bf16[2048,1024]{1,0:T(8,128)(2,1)}) %all-gather.5.cloned.1.call-update) | async-done | bytes 4194320 | tf_op jit(solution)/shard_map/all_gather | solution.py:171
  114.0 67.5 %all-gather.7.cloned.1.call-done = bf16[1024,512]{1,0:T(8,128)(2,1)} async-done(((bf16[64,512]{1,0:T(8,128)(2,1)}), bf16[1024,512]{1,0:T(8,128)(2,1)}) %all-gather.7.cloned.1.call-update) | async-done | bytes 1048592 | tf_op jit(solution)/shard_map/all_gather | solution.py:148
  181.5 11.7 %collective-permute-start.2 = (bf16[1024,512]{1,0:T(8,128)(2,1)}, bf16[1024,512]{1,0:T(8,128)(2,1)}, u32[]{:S(2)}, u32[]{:S(2)}) collective-permute-start(bf16[1024,512]{1,0:T(8,128)(2,1)} %all-gather.7.cloned.1.call-done), channel_id=1, source_target_pairs={{0,16},{16,0},{1,17},{17,1},{2,18},{18,2},{3,19},{19,3},{4,20},{20... | collective-permute-start | bytes 3145736 | tf_op jit(solution)/shard_map/ppermute | solution.py:36
  201.2 3.8 all-to-all-start
  205.0 54.0 %all-gather.9.cloned.1.call-done = bf16[3072,512]{1,0:T(8,128)(2,1)} async-done(((bf16[192,512]{1,0:T(8,128)(2,1)}), bf16[3072,512]{1,0:T(8,128)(2,1)}) %all-gather.9.cloned.1.call-update) | async-done | bytes 3145744 | tf_op jit(solution)/shard_map/all_gather | solution.py:190
  259.0 9.8 %collective-permute-start.3 = (bf16[3072,512]{1,0:T(8,128)(2,1)}, bf16[3072,512]{1,0:T(8,128)(2,1)}, u32[]{:S(2)}, u32[]{:S(2)}) collective-permute-start(bf16[3072,512]{1,0:T(8,128)(2,1)} %all-gather.9.cloned.1.call-done), channel_id=1, source_target_pairs={{0,16},{16,0},{1,17},{17,1},{2,18},{18,2},{3,19},{19,3},{4,20},{20... | collective-permute-start | bytes 9437192 | tf_op jit(solution)/shard_map/ppermute | solution.py:36
  271.7 3.7 convolution_convert_fusion
  276.8 20.8 %attend.1 = bf16[256,2048]{1,0:T(8,128)(2,1)} custom-call(bf16[2048,192]{1,0:T(8,128)(2,1)} %copy.52.qkv_ref, bf16[2048,64]{1,0:T(8,128)(2,1)} %bitcast.115), custom_call_target="tpu_custom_call" | custom-call | flops 6442450944 | bytes 2621440 | tf_op jit(solution)/shard_map/attend/pallas_call | solution.py:93
  299.8 4.1 all-to-all-start.1
  304.0 19.7 %all-to-all-done.1 = bf16[16,192,128]{2,1,0:T(8,128)(2,1)S(1)} async-done(((bf16[16,192,128]{2,1,0:T(8,128)(2,1)}), bf16[16,192,128]{2,1,0:T(8,128)(2,1)S(1)}, u32[]{:S(2)}, u32[]{:S(2)}) %all-to-all-start.1) | async-done | bytes 786464 | tf_op jit(solution)/shard_map/all_to_all | solution.py:193
  335.7 3.9 collective-permute-done.5
  340.7 3.6 gather_fusion.1
  344.4 5.1 %multiply_multiply_fusion = f32[768,1024]{1,0:T(8,128)S(1)} fusion(bf16[1024,1024]{1,0:T(8,128)(2,1)S(1)} %copy-done, f32[768,1024]{1,0:T(8,128)} %gather_fusion, f32[768]{0:T(1024)S(1)} %copy-done.12, f32[1024]{0:T(1024)S(1)} %bitcast.122, f32[768]{0:T(1024)S(1)} %get-tuple-element.47, f32[1024]{0:T(1024)S(1)} %bitcast.124, f32[768]{0:T(1024)S(1)} %get-tuple-element.48, ...), kind=kOutput, calls=%fused_computation.9 | convolution fusion | flops 1626341376 | bytes 9993216 | tf_op jit(solution)/shard_map/dot_general | solution.py:26
  354.1 4.0 collective-permute-start.6
  363.3 60.7 %all_to_all.25 = bf16[8,144,1024]{2,1,0:T(8,128)(2,1)S(1)} all-to-all(bf16[8,144,1024]{2,1,0:T(8,128)(2,1)S(1)} %pad_maximum_fusion), channel_id=1, replica_groups=mesh['dp_0'=2,'dp_1'=4,'dp_2'=2,'mp_0'=2,'mp_1'=8] {'dp_0','dp_1'}, dimensions={0} | all-to-all | bytes 4718592 | tf_op jit(solution)/shard_map/all_to_all | solution.py:248
  426.5 3.6 all-to-all-start.3
  441.0 6.9 %all-to-all-start.4 = ((bf16[16,64,256]{2,1,0:T(8,128)(2,1)}), bf16[16,64,256]{2,1,0:T(8,128)(2,1)S(1)}, u32[]{:S(2)}, u32[]{:S(2)}) async-start(bf16[16,64,256]{2,1,0:T(8,128)(2,1)} %pad_maximum_fusion.3), calls=%async_computation.4 | async-start | bytes 1048576 | tf_op jit(solution)/shard_map/all_to_all | solution.py:227
  452.4 6.5 %all-to-all-done.4 = bf16[16,64,256]{2,1,0:T(8,128)(2,1)S(1)} async-done(((bf16[16,64,256]{2,1,0:T(8,128)(2,1)}), bf16[16,64,256]{2,1,0:T(8,128)(2,1)S(1)}, u32[]{:S(2)}, u32[]{:S(2)}) %all-to-all-start.4) | async-done | bytes 524320 | tf_op jit(solution)/shard_map/all_to_all | solution.py:227
  (141 shorter events, 69.3 us)
Async XLA Ops:
  7.2 14.4 %copy-start = (bf16[1024,1024]{1,0:T(8,128)(2,1)S(1)}, bf16[1024,1024]{1,0:T(8,128)(2,1)}, u32[]{:S(2)}) copy-start(bf16[1024,1024]{1,0:T(8,128)(2,1)} %param.20) | copy-start | bytes 6291460
  7.2 106.8 %all-gather.5.cloned.1.call-start = ((), (), s32[]{:S(2)}) async-start(), calls=%async_computation.5 | async-start | bytes 4456448 | tf_op jit(solution)/shard_map/all_gather | solution.py:171
  9.0 8.4 %copy-start.14 = (f32[1,1024]{1,0:T(1,128)}, f32[1,1024]{1,0:T(1,128)S(1)}, u32[]{:S(2)}) copy-start(f32[1,1024]{1,0:T(1,128)S(1)} %get-tuple-element.69) | copy-start | bytes 12292
  21.6 20.0 %copy-start.9 = (bf16[1,128,1024]{2,1,0:T(8,128)(2,1)S(1)}, bf16[1,128,1024]{2,1,0:T(8,128)(2,1)}, u32[]{:S(2)}) copy-start(bf16[1,128,1024]{2,1,0:T(8,128)(2,1)} %param.13) | copy-start | bytes 786436
  26.9 18.4 %copy-start.8 = (bf16[3,1024,64]{1,2,0:T(8,128)(2,1)S(1)}, bf16[3,1024,64]{1,2,0:T(8,128)(2,1)}, u32[]{:S(2)}) copy-start(bf16[3,1024,64]{1,2,0:T(8,128)(2,1)} %param.21) | copy-start | bytes 1179652
  26.9 166.2 %copy-start.2 = (bf16[1,128,1024]{2,1,0:T(8,128)(2,1)S(1)}, bf16[1,128,1024]{2,1,0:T(8,128)(2,1)}, u32[]{:S(2)}) copy-start(bf16[1,128,1024]{2,1,0:T(8,128)(2,1)} %param.23) | copy-start | bytes 786436
  28.1 9.3 %collective-permute-start = (bf16[128,1024]{1,0:T(8,128)(2,1)S(1)}, bf16[128,1024]{1,0:T(8,128)(2,1)S(1)}, u32[]{:S(2)}, u32[]{:S(2)}) collective-permute-start(bf16[128,1024]{1,0:T(8,128)(2,1)S(1)} %get-tuple-element.54), channel_id=1, source_target_pairs={{0,1},{1,2},{2,3},{3,4},{4,5},{5,6},{6,7},{7,8},{8,9},{9,10},{10,1... | collective-permute-start | bytes 786440 | tf_op jit(solution)/shard_map/ppermute | solution.py:32
  32.5 9.1 %collective-permute-start.1 = (bf16[128,1024]{1,0:T(8,128)(2,1)S(1)}, bf16[128,1024]{1,0:T(8,128)(2,1)S(1)}, u32[]{:S(2)}, u32[]{:S(2)}) collective-permute-start(bf16[128,1024]{1,0:T(8,128)(2,1)S(1)} %get-tuple-element.55), channel_id=1, source_target_pairs={{1,0},{2,1},{3,2},{4,3},{5,4},{6,5},{7,6},{8,7},{9,8},{10,9},{11,1... | collective-permute-start | bytes 786440 | tf_op jit(solution)/shard_map/ppermute | solution.py:32
  42.9 152.0 %copy-start.25 = (f32[128]{0:T(128)}, f32[128]{0:T(128)S(1)}, u32[]{:S(2)}) copy-start(f32[128]{0:T(128)S(1)} %add_rsqrt_fusion) | copy-start | bytes 1540
  43.7 137.8 %all-gather.7.cloned.1.call-start = ((), (), s32[]{:S(2)}) async-start(), calls=%async_computation.6 | async-start | bytes 1114112 | tf_op jit(solution)/shard_map/all_gather | solution.py:148
  45.3 213.7 %all-gather.9.cloned.1.call-start = ((), (), s32[]{:S(2)}) async-start(), calls=%async_computation.7 | async-start | bytes 3342336 | tf_op jit(solution)/shard_map/all_gather | solution.py:190
  181.5 14.3 %collective-permute-start.2 = (bf16[1024,512]{1,0:T(8,128)(2,1)}, bf16[1024,512]{1,0:T(8,128)(2,1)}, u32[]{:S(2)}, u32[]{:S(2)}) collective-permute-start(bf16[1024,512]{1,0:T(8,128)(2,1)} %all-gather.7.cloned.1.call-done), channel_id=1, source_target_pairs={{0,16},{16,0},{1,17},{17,1},{2,18},{18,2},{3,19},{19,3},{4,20},{20... | collective-permute-start | bytes 3145736 | tf_op jit(solution)/shard_map/ppermute | solution.py:36
  201.2 69.3 %all-to-all-start = ((bf16[16,64,128]{2,1,0:T(8,128)(2,1)}), bf16[16,64,128]{2,1,0:T(8,128)(2,1)S(1)}, u32[]{:S(2)}, u32[]{:S(2)}) async-start(bf16[16,64,128]{2,1,0:T(8,128)(2,1)} %reshape.131), calls=%async_computation | async-start | bytes 524288 | tf_op jit(solution)/shard_map/all_to_all | solution.py:179
  259.0 67.2 %collective-permute-start.3 = (bf16[3072,512]{1,0:T(8,128)(2,1)}, bf16[3072,512]{1,0:T(8,128)(2,1)}, u32[]{:S(2)}, u32[]{:S(2)}) collective-permute-start(bf16[3072,512]{1,0:T(8,128)(2,1)} %all-gather.9.cloned.1.call-done), channel_id=1, source_target_pairs={{0,16},{16,0},{1,17},{17,1},{2,18},{18,2},{3,19},{19,3},{4,20},{20... | collective-permute-start | bytes 9437192 | tf_op jit(solution)/shard_map/ppermute | solution.py:36
  299.8 23.8 %all-to-all-start.1 = ((bf16[16,192,128]{2,1,0:T(8,128)(2,1)}), bf16[16,192,128]{2,1,0:T(8,128)(2,1)S(1)}, u32[]{:S(2)}, u32[]{:S(2)}) async-start(bf16[16,192,128]{2,1,0:T(8,128)(2,1)} %bitcast_bitcast_fusion), calls=%async_computation.1 | async-start | bytes 1572864 | tf_op jit(solution)/shard_map/all_to_all | solution.py:193
  303.9 129.7 %all-gather.11.cloned.1.call-start = ((), (), s32[]{:S(2)}) async-start(), calls=%async_computation.8 | async-start | bytes 4456448 | tf_op jit(solution)/shard_map/all_gather | solution.py:197
  329.1 15.2 %copy-start.7 = (bf16[128,1024]{1,0:T(8,128)(2,1)}, bf16[128,1024]{1,0:T(8,128)(2,1)S(1)}, u32[]{:S(2)}) copy-start(bf16[128,1024]{1,0:T(8,128)(2,1)S(1)} %subtract_convert_fusion) | copy-start | bytes 786436
  329.1 6.6 %collective-permute-start.4 = (bf16[128,1024]{1,0:T(8,128)(2,1)S(1)}, bf16[128,1024]{1,0:T(8,128)(2,1)S(1)}, u32[]{:S(2)}, u32[]{:S(2)}) collective-permute-start(bf16[128,1024]{1,0:T(8,128)(2,1)S(1)} %subtract_convert_fusion), channel_id=1, source_target_pairs={{0,1},{1,2},{2,3},{3,4},{4,5},{5,6},{6,7},{7,8},{8,9},{9,10},{10,1... | collective-permute-start | bytes 786440 | tf_op jit(solution)/shard_map/ppermute | solution.py:32
  332.4 7.2 %collective-permute-start.5 = (bf16[128,1024]{1,0:T(8,128)(2,1)S(1)}, bf16[128,1024]{1,0:T(8,128)(2,1)}, u32[]{:S(2)}, u32[]{:S(2)}) collective-permute-start(bf16[128,1024]{1,0:T(8,128)(2,1)S(1)} %subtract_convert_fusion), channel_id=1, source_target_pairs={{1,0},{2,1},{3,2},{4,3},{5,4},{6,5},{7,6},{8,7},{9,8},{10,9},{11,1... | collective-permute-start | bytes 786440 | tf_op jit(solution)/shard_map/ppermute | solution.py:32
  354.1 7.9 %collective-permute-start.6 = (bf16[8,2,64,1024]{3,2,1,0:T(8,128)(2,1)S(1)}, bf16[8,2,64,1024]{3,2,1,0:T(8,128)(2,1)S(1)}, u32[]{:S(2)}, u32[]{:S(2)}) collective-permute-start(bf16[8,2,64,1024]{3,2,1,0:T(8,128)(2,1)S(1)} %bitcast.108), channel_id=1, source_target_pairs={{0,16},{16,0},{1,17},{17,1},{2,18},{18,2},{3,19},{19,3},{4,20},{20... | collective-permute-start | bytes 6291464 | tf_op jit(solution)/shard_map/ppermute | solution.py:36
  359.9 2.1 collective-permute-start.7
  426.5 14.6 %all-to-all-start.3 = ((bf16[16,96,128]{2,1,0:T(8,128)(2,1)}), bf16[16,96,128]{2,1,0:T(8,128)(2,1)S(1)}, u32[]{:S(2)}, u32[]{:S(2)}) async-start(bf16[16,96,128]{2,1,0:T(8,128)(2,1)} %pad_maximum_fusion.4), calls=%async_computation.3 | async-start | bytes 786432 | tf_op jit(solution)/shard_map/all_to_all | solution.py:258
  437.7 22.8 %copy-start.1 = (bf16[1024,1024]{1,0:T(8,128)(2,1)S(1)}, bf16[1024,1024]{1,0:T(8,128)(2,1)}, u32[]{:S(2)}) copy-start(bf16[1024,1024]{1,0:T(8,128)(2,1)} %param.20) | copy-start | bytes 6291460
  441.0 17.9 %all-to-all-start.4 = ((bf16[16,64,256]{2,1,0:T(8,128)(2,1)}), bf16[16,64,256]{2,1,0:T(8,128)(2,1)S(1)}, u32[]{:S(2)}, u32[]{:S(2)}) async-start(bf16[16,64,256]{2,1,0:T(8,128)(2,1)} %pad_maximum_fusion.3), calls=%async_computation.4 | async-start | bytes 1048576 | tf_op jit(solution)/shard_map/all_to_all | solution.py:227
  (19 other events, 85.4 us)
Sparse Core Ops, SparseCore 0:
  43.8 70.0 all-gather.4
  116.3 65.1 all-gather.6
  183.3 75.6 all-gather.8
  334.1 83.1 all-gather.10

commit v2 on v1

--- a/solution.py
+++ b/solution.py
@@ -51,13 +51,20 @@
     return lax.dynamic_slice_in_dim(value, half * width, width, 1)
 
 
-def attend_kernel(qkv_ref, da_ref, out_ref, k_s, v_s, kt_s, vt_s, dk_s, dv_s, *, block, steps):
+def attend_kernel(
+    half_ref, qkvd_ref, out_ref, sent_ref, k_s, v_s, kt_s, vt_s, dk_s, dv_s, *, block, steps, nodes
+):
     i = pl.program_id(0)
+    along = block * steps // nodes // 2
+
+    def place(b):
+        position = (b % along) * 2 + (b // along + half_ref[0]) % 2
+        return pl.ds(pl.multiple_of(position * nodes, nodes), nodes)
 
     @pl.when(i == 0)
     def _():
-        k = qkv_ref[:, HDIM : 2 * HDIM]
-        v = qkv_ref[:, 2 * HDIM : 3 * HDIM]
+        k = qkvd_ref[:, HDIM : 2 * HDIM]
+        v = qkvd_ref[:, 2 * HDIM : 3 * HDIM]
         k_s[...] = k
         v_s[...] = v
         kt_s[...] = k.T
@@ -66,8 +73,8 @@
         dv_s[...] = jnp.zeros_like(dv_s)
 
     rows = pl.ds(pl.multiple_of(i * block, block), block)
-    q = qkv_ref[rows, 0:HDIM] * jnp.asarray(SCALE, BF)
-    da = da_ref[rows, :]
+    q = qkvd_ref[rows, 0:HDIM] * jnp.asarray(SCALE, BF)
+    da = qkvd_ref[rows, 3 * HDIM : 4 * HDIM]
     s = dot(k_s[...], q, NT)
     dp = dot(v_s[...], da, NT)
     e = jnp.exp(s - jnp.max(s, axis=0, keepdims=True))
@@ -75,30 +82,47 @@
     delta = jnp.sum(p * dp, axis=0, keepdims=True)
     pb = p.astype(BF)
     ds = (p * (dp - delta)).astype(BF)
-    out_ref[3 * HDIM : 4 * HDIM, rows] = dot(vt_s[...], pb, NN).astype(BF)
-    out_ref[0:HDIM, rows] = (dot(kt_s[...], ds, NN) * SCALE).astype(BF)
+    attended = dot(vt_s[...], pb, NN).astype(BF)
+    dq = (dot(kt_s[...], ds, NN) * SCALE).astype(BF)
+    for j in range(block // nodes):
+        b = i * (block // nodes) + j
+        cols = slice(j * nodes, (j + 1) * nodes)
+        sent_ref[b, 0:HDIM, :] = dq[:, cols]
+        out_ref[0:HDIM, place(b)] = dq[:, cols]
+        out_ref[3 * HDIM : 4 * HDIM, place(b)] = attended[:, cols]
     dk_s[...] += dot(ds, q, NN)
     dv_s[...] += dot(pb, da, NN)
 
     @pl.when(i == steps - 1)
     def _():
-        out_ref[HDIM : 2 * HDIM, :] = dk_s[...].T.astype(BF)
-        out_ref[2 * HDIM : 3 * HDIM, :] = dv_s[...].T.astype(BF)
-
-
-def attend(qkv, da):
-    total = qkv.shape[0]
+        dk = dk_s[...].T.astype(BF)
+        dv = dv_s[...].T.astype(BF)
+        for b in range(block * steps // nodes):
+            cols = slice(b * nodes, (b + 1) * nodes)
+            for first, value in ((HDIM, dk[:, cols]), (2 * HDIM, dv[:, cols])):
+                sent_ref[b, first : first + HDIM, :] = value
+                out_ref[first : first + HDIM, place(b)] = value
+
+
+def attend(qkvd, half, nodes):
+    total = qkvd.shape[0]
     block = min(512, total)
     steps = total // block
     return pl.pallas_call(
-        functools.partial(attend_kernel, block=block, steps=steps),
+        functools.partial(attend_kernel, block=block, steps=steps, nodes=nodes),
         grid=(steps,),
         in_specs=[
-            pl.BlockSpec((total, 3 * HDIM), lambda i: (0, 0)),
-            pl.BlockSpec((total, HDIM), lambda i: (0, 0)),
-        ],
-        out_specs=pl.BlockSpec((4 * HDIM, total), lambda i: (0, 0)),
-        out_shape=jax.ShapeDtypeStruct((4 * HDIM, total), BF),
+            pl.BlockSpec(memory_space=pltpu.SMEM),
+            pl.BlockSpec((total, 4 * HDIM), lambda i: (0, 0)),
+        ],
+        out_specs=[
+            pl.BlockSpec((4 * HDIM, total), lambda i: (0, 0)),
+            pl.BlockSpec((total // nodes, 3 * HDIM, nodes), lambda i: (0, 0, 0)),
+        ],
+        out_shape=[
+            jax.ShapeDtypeStruct((4 * HDIM, total), BF),
+            jax.ShapeDtypeStruct((total // nodes, 3 * HDIM, nodes), BF),
+        ],
         scratch_shapes=[
             pltpu.VMEM((total, HDIM), BF),
             pltpu.VMEM((total, HDIM), BF),
@@ -114,7 +138,7 @@
             bytes_accessed=20 * total * HDIM,
         ),
         name="attend",
-    )(qkv, da)
+    )(half.reshape(1), qkvd)
 
 
 def shards(
@@ -145,8 +169,12 @@
     source_local = edge_source[0] - band * grid_rows
     dest_local = edge_dest[0] - (band - 1) * nodes
 
-    o_mine = lax.all_gather(column_half(w_o, core), MP, axis=0, tiled=True)
-    o_other = swapped(o_mine)
+    width = w_qkv.shape[2]
+    upper = lax.axis_index("dp_0")
+    w_rows = jnp.concatenate([w_qkv.transpose(0, 2, 1).reshape(3 * width, channels), w_o], axis=0)
+    w_part = lax.dynamic_slice_in_dim(column_half(w_rows, core), upper * 2 * width, 2 * width, 0)
+    w_mine = lax.all_gather(w_part, ("dp_0",) + MP, axis=0, tiled=True)
+    cot_beside = lax.ppermute(cot, "mp_0", [(0, 1), (1, 0)])
 
     projected = dot(grid, w_in, NN)
     attr_columns = edge_attr[0].T
@@ -168,33 +196,37 @@
     )
     inv = lax.rsqrt(jnp.mean(node * node, axis=-1, keepdims=True) + EPS)
     normed = (node * inv).astype(BF)
-    all_normed = lax.all_gather(normed, MP, axis=0, tiled=True)
-
-    d_att = (
-        dot(column_half(cot, core), o_mine, NT) + dot(column_half(cot, 1 - core), o_other, NT)
-    ).astype(BF)
-    width = w_qkv.shape[2]
-    d_att = d_att.reshape(2, nodes // 2, bands, width).transpose(2, 1, 0, 3)
-    d_att = d_att.reshape(bands, nodes // 2, 2 * width)
-    d_att = lax.all_to_all(d_att, MP, 0, 0, tiled=True)
-    d_att = d_att.reshape(bands, nodes // 2, 2, width).transpose(0, 2, 1, 3)
-    d_att = d_att.reshape(bands * nodes, width)
-
-    w_rows = jnp.concatenate([w_qkv[0], w_qkv[1], w_qkv[2]], axis=1)
-    qkv = dot(all_normed, w_rows, NN).astype(BF)
-    result = attend(qkv, d_att)
-    dqkv = result[: 3 * width]
-
-    w_heads = w_qkv.transpose(0, 2, 1).reshape(3 * width, channels)
-    w_half = after(column_half(w_heads, core), all_normed)
-    w_mine = lax.all_gather(w_half, MP, axis=0, tiled=True)
+
+    normed_beside = lax.ppermute(normed, "mp_0", [(0, 1), (1, 0)])
+    w_mine = after(w_mine, normed_beside)
     w_other = swapped(w_mine)
-    pieces = dqkv.reshape(3 * width, bands, nodes).transpose(1, 0, 2)
+    both = jnp.concatenate([normed, cot], axis=0)
+    heads = dot(column_half(both, core), w_mine, NT) + dot(column_half(both, 1 - core), w_other, NT)
+    column = lax.broadcasted_iota(jnp.int32, (nodes, heads.shape[1]), 1)
+    of_output = (column >= 2 * width * bands) & (column % (2 * width) >= width)
+    heads = jnp.where(of_output, heads[nodes:], heads[:nodes]).astype(BF)
+    heads = heads.reshape(nodes, 2, bands, 2 * width).transpose(2, 0, 1, 3)
+    heads = heads.reshape(bands, nodes, 4 * width)
+    heads = lax.all_to_all(heads, MP, 0, 0, tiled=True).reshape(bands * nodes, 4 * width)
+
+    wide = jnp.concatenate([normed, cot], axis=1)
+    beside = jnp.concatenate([normed_beside, cot_beside], axis=1)
+    wide = after(jnp.concatenate([wide, beside], axis=0), w_mine)
+    wide = lax.all_gather(wide, "mp_1", axis=0, tiled=True)
+
+    result, pieces = attend(heads, lax.axis_index("mp_0"), nodes)
+
     pieces = lax.all_to_all(pieces, MP, 0, 0, tiled=True)
     pieces = pieces.reshape(bands * 3 * width, nodes)
-    dx = both_halves(dot(pieces, w_mine, TN), dot(pieces, w_other, TN), core)
-
-    all_cot = lax.all_gather(after(cot, w_mine), MP, axis=0, tiled=True)
+
+    def only_qkv(rows):
+        rows = rows.reshape(2, bands, 2 * width, -1)
+        rows = jnp.concatenate([rows[0], rows[1, :, :width]], axis=1)
+        return rows.reshape(bands * 3 * width, -1)
+
+    dx = both_halves(
+        dot(pieces, only_qkv(w_mine), TN), dot(pieces, only_qkv(w_other), TN), core
+    )
 
     dnode = (
         cot.astype(F32)
@@ -220,24 +252,26 @@
     dw_in = dot(grid, dproj, TN).astype(BF)
     d_grid = dot(dproj, w_in, NT).astype(BF)
 
-    dw_x = dot(all_normed, dqkv, (((0,), (1,)), ((), ())))
-    dw_c = dot(all_cot, result[3 * width :], (((0,), (1,)), ((), ())))
-    dw_heads = jnp.concatenate([dw_x, dw_c], axis=1).astype(BF)
-    dw_heads = dw_heads.reshape(2 * groups, -1, 4 * width)
-    dw_heads = lax.all_to_all(dw_heads, DP, 0, 0, tiled=True)
-    sum_heads = jnp.sum(dw_heads.astype(F32), axis=0)
-    sum_qkv = jnp.stack([sum_heads[:, j * width : (j + 1) * width] for j in range(3)])
-    sum_o = sum_heads[:, 3 * width :].T
+    dw_heads = dot(wide, result, (((0,), (1,)), ((), ()))).astype(BF)
+    of_output = lax.broadcasted_iota(jnp.int32, (channels, 4 * width), 1) >= 3 * width
+    dw_heads = jnp.where(of_output, dw_heads[channels:], dw_heads[:channels])
 
     rows = channels // (2 * groups)
-    both = jnp.stack(
-        [dw_in.reshape(groups, 2, rows, channels), dw_out.reshape(groups, 2, rows, channels)],
+    folded = 4 * width * rows // channels
+    dw_heads = dw_heads.reshape(groups, 2, rows // folded, folded, 4 * width)
+    dw_heads = dw_heads.transpose(0, 1, 3, 2, 4).reshape(groups, 2, folded, channels)
+    both = jnp.concatenate(
+        [
+            dw_in.reshape(groups, 2, rows, channels),
+            dw_out.reshape(groups, 2, rows, channels),
+            dw_heads,
+        ],
         axis=2,
     )
     mine = lax.dynamic_index_in_dim(both, core, 1, keepdims=False)
     theirs = lax.dynamic_index_in_dim(both, 1 - core, 1, keepdims=False)
     pair = mine.astype(F32) + swapped(theirs).astype(F32)
-    pair = pair.astype(BF).reshape(groups, 2 * rows, channels)
+    pair = pair.astype(BF)
     attr = dw_attr + swapped(dw_attr)
     attr_rows = attr.shape[0]
     attr_high = attr.astype(BF)
@@ -247,8 +281,13 @@
     pair = jnp.concatenate([pair, jnp.broadcast_to(tail[None], (groups, 16, channels))], axis=1)
     pair = lax.all_to_all(pair, GROUP, 0, 0, tiled=True)
     summed = jnp.sum(pair.astype(F32), axis=0)
-    attr = summed[2 * rows : 2 * rows + attr_rows]
-    attr = attr + summed[2 * rows + attr_rows : 2 * rows + 2 * attr_rows]
+    sum_heads = summed[2 * rows : 2 * rows + folded]
+    sum_heads = sum_heads.reshape(folded, rows // folded, 4 * width).transpose(1, 0, 2)
+    sum_heads = sum_heads.reshape(rows, 4 * width)
+    sum_qkv = jnp.stack([sum_heads[:, j * width : (j + 1) * width] for j in range(3)])
+    sum_o = sum_heads[:, 3 * width :].T
+    first = 2 * rows + folded
+    attr = summed[first : first + attr_rows] + summed[first + attr_rows : first + 2 * attr_rows]
     cols = channels // bands
     blocks = summed[: 2 * rows].astype(BF).reshape(2, rows, bands, cols)
     blocks = blocks.transpose(2, 1, 0, 3).reshape(bands, rows, 2 * cols)

time: 468 us -> 340 us (0.73)
  waiting for transfers between devices: 233 us -> 82 us
  blocking collectives: 60.7 us -> 83.9 us
  starting transfers between devices: 54.8 us -> 45.1 us
  local copies, waits for them, and re-layouts: 28 us -> 33.6 us
    all_gather x4 -> x2, waiting for transfers between devices: 189 us -> 37.2 us  [the longest x1 37.2 us: shards(): w_mine = lax.all_gather(w_part, ('dp_0',) + MP, axis=0, tiled=True)]
    all_to_all x0 -> x1, blocking collectives: none -> 43.4 us  [shards(): lax.all_to_all(heads, MP, 0, 0, tiled=True)]
    all_to_all x1, blocking collectives: 60.7 us -> 40.4 us  [shards(): pair = lax.all_to_all(pair, GROUP, 0, 0, tiled=True)]
    ppermute x4 -> x3, starting transfers between devices: 25.9 us -> 7.09 us  [swapped(): return lax.ppermute(block, CORE, [(0, 1), (1, 0)])]
    ppermute x0 -> x2, starting transfers between devices: none -> 15.3 us  [the longest x1 10.1 us: shards(): normed_beside = lax.ppermute(normed, 'mp_0', [(0, 1), (1, 0)])]
    all_to_all x2 -> x0, starting transfers between devices: 10.7 us -> none  [the longest x1 6.9 us: shards(): dw_heads = lax.all_to_all(dw_heads, DP, 0, 0, tiled=True)]
    ppermute x4, waiting for transfers between devices: 13.5 us -> 6.16 us  [shifted(): return lax.ppermute(block, axis, route)]
    all_to_all x2 -> x0, waiting for transfers between devices: 6.49 us -> none  [the longest x1 6.49 us: shards(): dw_heads = lax.all_to_all(dw_heads, DP, 0, 0, tiled=True)]
  transfers between devices with their start and end apart: 16 -> 13, of which waited for: 12 -> 7; matrix products, arithmetic and copies ran while one was open for 12% -> 20% of each run, Pallas kernels for 4% -> 6%
where the time goes in v2:
time: 340 us; the launch traced here: 338 us
  blocking collectives  83.9 us (25%)
  waiting for transfers between devices  82 us (24%)
  starting transfers between devices  45.1 us (13%)
  matrix products  38.6 us (11%)
  local copies, waits for them, and re-layouts  33.6 us (10%)
  Pallas kernels  21 us (6%)
  other arithmetic  18.4 us (5%)
  between operations  15.2 us (4%)
    all_to_all x1, blocking collectives, shards(): lax.all_to_all(heads, MP, 0, 0, tiled=True)  43.4 us
    all_to_all x1, blocking collectives, shards(): pair = lax.all_to_all(pair, GROUP, 0, 0, tiled=True)  40.4 us
    all_gather x1, waiting for transfers between devices, shards(): w_mine = lax.all_gather(w_part, ('dp_0',) + MP, axis=0, tiled=True)  37.2 us
    dot_general x12, matrix products, dot(): return lax.dot_general(a, b, dims, preferred_element_type=F32)  36.9 us
    pallas_call x1, Pallas kernels, attend(): pl.pallas_call(functools.partial(attend_kernel, block=block, steps=steps,...  21 us
    all_to_all x1, waiting for transfers between devices, shards(): pieces = lax.all_to_all(pieces, MP, 0, 0, tiled=True)  19.5 us
    ppermute x4, starting transfers between devices, shifted(): return lax.ppermute(block, axis, route)  12.3 us
    ppermute x1, starting transfers between devices, shards(): normed_beside = lax.ppermute(normed, 'mp_0', [(0, 1), (1, 0)])  10.1 us
  transfers between devices with their start and end apart: 13, of which 7 were waited for; matrix products, arithmetic and copies ran while one was open for 20% of the time, Pallas kernels for 6%

profile of v2, /device:TPU:1, one launch (start us, length us, event | category | flops | bytes accessed | tf_op | source)
XLA Modules:
  0.0 337.7 jit_solution(16021947138417851084)
XLA Ops:
  13.1 3.6 %gather_fusion = f32[768,1024]{1,0:T(8,128)} fusion(f32[256,1024]{1,0:T(8,128)S(1)} %fusion.29, s32[1024]{0:T(1024)S(1)} %pad_clamp_fusion.1), kind=kCustom, calls=%fused_computation | custom fusion | bytes 6294528 | tf_op jit(solution)/shard_map/gather | solution.py:184
  16.9 4.1 %multiply_convert_fusion.1 = bf16[768,1024]{1,0:T(8,128)(2,1)} fusion(f32[768,1024]{1,0:T(8,128)} %gather_fusion, f32[768]{0:T(1024)S(1)} %fusion.44, f32[1024]{0:T(1024)S(1)} %bitcast.119, f32[768]{0:T(1024)S(1)} %get-tuple-element.30, f32[1024]{0:T(1024)S(1)} %bitcast.121, f32[768]{0:T(1024)S(1)} %get-tuple-element.31, f32[1024]{0:T(1024)S(1)} %bitcast.117, ...), kind=kLoop, calls=%fused_computation.17 | loop fusion | flops 11010048 | bytes 4750336 | tf_op jit(solution)/shard_map/convert_element_type | solution.py:185
  21.0 5.3 %fusion.57 = (bf16[384,1024]{1,0:T(8,128)(2,1)}, f32[384,1024]{1,0:T(8,128)}) fusion(bf16[768,1024]{1,0:T(8,128)(2,1)} %multiply_convert_fusion.1, bf16[1024,1024]{1,0:T(8,128)(2,1)S(1)} %copy-done, s32[768]{0:T(1024)S(1)} %subtract_reduce_fusion), kind=kOutput, calls=%fused_computation.119 | convolution fusion | flops 2216067072 | bytes 6032384 | tf_op jit(solution)/shard_map/dot_general | solution.py:26
  28.7 5.0 %collective-permute-start = (bf16[128,1024]{1,0:T(8,128)(2,1)S(1)}, bf16[128,1024]{1,0:T(8,128)(2,1)S(1)}, u32[]{:S(2)}, u32[]{:S(2)}) collective-permute-start(bf16[128,1024]{1,0:T(8,128)(2,1)S(1)} %get-tuple-element.35), channel_id=1, source_target_pairs={{0,1},{1,2},{2,3},{3,4},{4,5},{5,6},{6,7},{7,8},{8,9},{9,10},{10,1... | collective-permute-start | bytes 786440 | tf_op jit(solution)/shard_map/ppermute | solution.py:32
  33.7 5.2 %collective-permute-start.6 = (bf16[128,1024]{1,0:T(8,128)(2,1)S(1)}, bf16[128,1024]{1,0:T(8,128)(2,1)S(1)}, u32[]{:S(2)}, u32[]{:S(2)}) collective-permute-start(bf16[128,1024]{1,0:T(8,128)(2,1)S(1)} %bitcast.99), channel_id=1, source_target_pairs={{0,8},{8,0},{1,9},{9,1},{2,10},{10,2},{3,11},{11,3},{4,12},{12,4},... | collective-permute-start | bytes 786440 | tf_op jit(solution)/shard_map/ppermute | solution.py:177
  40.3 10.1 %collective-permute-start.2 = (bf16[128,1024]{1,0:T(8,128)(2,1)S(1)}, bf16[128,1024]{1,0:T(8,128)(2,1)S(1)}, u32[]{:S(2)}, u32[]{:S(2)}) collective-permute-start(bf16[128,1024]{1,0:T(8,128)(2,1)S(1)} %multiply_convert_fusion.4), channel_id=1, source_target_pairs={{0,8},{8,0},{1,9},{9,1},{2,10},{10,2},{3,11},{11,3},{4,12},{12,4},... | collective-permute-start | bytes 786440 | tf_op jit(solution)/shard_map/ppermute | solution.py:200
  50.4 4.7 %collective-permute-done.2 = bf16[128,1024]{1,0:T(8,128)(2,1)S(1)} collective-permute-done((bf16[128,1024]{1,0:T(8,128)(2,1)S(1)}, bf16[128,1024]{1,0:T(8,128)(2,1)S(1)}, u32[]{:S(2)}, u32[]{:S(2)}) %collective-permute-start.2) | collective-permute-done | bytes 262176 | tf_op jit(solution)/shard_map/ppermute | solution.py:200
  56.2 37.2 %all-gather.3.cloned.1.call-done = bf16[4096,512]{1,0:T(8,128)(2,1)} async-done(((bf16[128,512]{1,0:T(8,128)(2,1)}), bf16[4096,512]{1,0:T(8,128)(2,1)}) %all-gather.3.cloned.1.call-update) | async-done | bytes 4194320 | tf_op jit(solution)/shard_map/all_gather | solution.py:176
  93.4 4.3 %collective-permute-start.3 = (bf16[4096,512]{1,0:T(8,128)(2,1)}, bf16[4096,512]{1,0:T(8,128)(2,1)}, u32[]{:S(2)}, u32[]{:S(2)}) collective-permute-start(bf16[4096,512]{1,0:T(8,128)(2,1)} %all-gather.3.cloned.1.call-done), channel_id=1, source_target_pairs={{0,16},{16,0},{1,17},{17,1},{2,18},{18,2},{3,19},{19,3},{4,20},{20... | collective-permute-start | bytes 12582920 | tf_op jit(solution)/shard_map/ppermute | solution.py:36
  97.7 7.1 %collective-permute-done.3 = bf16[4096,512]{1,0:T(8,128)(2,1)} collective-permute-done((bf16[4096,512]{1,0:T(8,128)(2,1)}, bf16[4096,512]{1,0:T(8,128)(2,1)}, u32[]{:S(2)}, u32[]{:S(2)}) %collective-permute-start.3) | collective-permute-done | bytes 4194336 | tf_op jit(solution)/shard_map/ppermute | solution.py:36
  104.8 3.5 %fusion.33 = f32[256,4096]{1,0:T(8,128)S(1)} fusion(bf16[4096,512]{1,0:T(8,128)(2,1)} %collective-permute-done.3, s32[]{:T(128)S(6)} %select_n.75, bf16[128,1024]{1,0:T(8,128)(2,1)S(1)} %multiply_convert_fusion.4, bf16[128,1024]{1,0:T(8,128)(2,1)S(1)} %bitcast.101), kind=kOutput, calls=%fused_computation.71 | convolution fusion | flops 1074266112 | bytes 8912900 | tf_op jit(solution)/shard_map/dot_general | solution.py:26
  114.8 43.4 %all_to_all.20 = bf16[16,128,256]{2,1,0:T(8,128)(2,1)} all-to-all(bf16[16,128,256]{2,1,0:T(8,128)(2,1)} %reshape.148), channel_id=1, replica_groups=mesh['dp_0'=2,'dp_1'=4,'dp_2'=2,'mp_0'=2,'mp_1'=8] {'mp_0','mp_1'}, dimensions={0} | all-to-all | bytes 2097152 | tf_op jit(solution)/shard_map/all_to_all | solution.py:210
  158.2 21.0 %attend.1 = (bf16[256,2048]{1,0:T(8,128)(2,1)}, bf16[16,192,128]{2,1,0:T(8,128)(2,1)}) custom-call(s32[1]{0:T(128)} %bitcast.12.half_ref, bf16[2048,256]{1,0:T(8,128)(2,1)} %bitcast.109), custom_call_target="tpu_custom_call" | custom-call | flops 6442450944 | bytes 2621440 | tf_op jit(solution)/shard_map/attend/pallas_call | solution.py:111
  179.2 4.3 %all-to-all-start.1 = ((bf16[16,192,128]{2,1,0:T(8,128)(2,1)}), bf16[16,192,128]{2,1,0:T(8,128)(2,1)}, u32[]{:S(2)}, u32[]{:S(2)}) async-start(bf16[16,192,128]{2,1,0:T(8,128)(2,1)} %get-tuple-element.12), calls=%async_computation.1 | async-start | bytes 1572864 | tf_op jit(solution)/shard_map/all_to_all | solution.py:219
  194.4 19.5 %all-to-all-done.1 = bf16[16,192,128]{2,1,0:T(8,128)(2,1)} async-done(((bf16[16,192,128]{2,1,0:T(8,128)(2,1)}), bf16[16,192,128]{2,1,0:T(8,128)(2,1)}, u32[]{:S(2)}, u32[]{:S(2)}) %all-to-all-start.1) | async-done | bytes 786464 | tf_op jit(solution)/shard_map/all_to_all | solution.py:219
  220.8 4.7 %collective-permute-start.4 = (bf16[128,1024]{1,0:T(8,128)(2,1)S(1)}, bf16[128,1024]{1,0:T(8,128)(2,1)}, u32[]{:S(2)}, u32[]{:S(2)}) collective-permute-start(bf16[128,1024]{1,0:T(8,128)(2,1)S(1)} %subtract_convert_fusion), channel_id=1, source_target_pairs={{0,1},{1,2},{2,3},{3,4},{4,5},{5,6},{6,7},{7,8},{8,9},{9,10},{10,1... | collective-permute-start | bytes 786440 | tf_op jit(solution)/shard_map/ppermute | solution.py:32
  225.5 6.1 %collective-permute-done.5 = bf16[128,1024]{1,0:T(8,128)(2,1)S(1)} collective-permute-done((bf16[128,1024]{1,0:T(8,128)(2,1)S(1)}, bf16[128,1024]{1,0:T(8,128)(2,1)S(1)}, u32[]{:S(2)}, u32[]{:S(2)}) %collective-permute-start.5) | collective-permute-done | bytes 262176 | tf_op jit(solution)/shard_map/ppermute | solution.py:32
  232.7 3.6 %gather_fusion.1 = bf16[768,1024]{1,0:T(8,128)(2,1)} fusion(bf16[384,1024]{1,0:T(8,128)(2,1)S(1)} %pad_maximum_fusion.2, s32[1024]{0:T(1024)S(1)} %pad_clamp_fusion), kind=kCustom, calls=%fused_computation.1 | custom fusion | bytes 3148800 | tf_op jit(solution)/shard_map/gather | solution.py:240
  236.2 5.1 %multiply_multiply_fusion = f32[768,1024]{1,0:T(8,128)S(1)} fusion(bf16[1024,1024]{1,0:T(8,128)(2,1)S(1)} %copy-done, f32[768,1024]{1,0:T(8,128)} %gather_fusion, f32[768]{0:T(1024)S(1)} %fusion.44, f32[1024]{0:T(1024)S(1)} %bitcast.120, f32[768]{0:T(1024)S(1)} %get-tuple-element.30, f32[1024]{0:T(1024)S(1)} %bitcast.122, f32[768]{0:T(1024)S(1)} %get-tuple-element.31, ...), kind=kOutput, calls=%fused_computation.15 | convolution fusion | flops 1626341376 | bytes 9993216 | tf_op jit(solution)/shard_map/dot_general | solution.py:26
  247.9 6.2 %convolution_convert_fusion = bf16[2048,256]{1,0:T(8,128)(2,1)S(1)} fusion(bf16[2048,2048]{1,0:T(8,128)(2,1)} %all-gather.5.cloned.1.call-done, bf16[256,2048]{1,0:T(8,128)(2,1)} %get-tuple-element.14), kind=kOutput, calls=%fused_computation.21 | convolution fusion | flops 2148007936 | bytes 10485760 | tf_op jit(solution)/shard_map/dot_general | solution.py:26
  264.6 3.5 %fusion = bf16[8,144,1024]{2,1,0:T(8,128)(2,1)S(1)} fusion(bf16[8,144,1024]{2,1,0:T(8,128)(2,1)} %collective-permute-done.7, bf16[8,2,144,1024]{3,2,1,0:T(8,128)(2,1)} %copy-done.2, s32[]{:T(128)S(6)} %select_n.81), kind=kLoop, calls=%fused_computation.6 | loop fusion | flops 4718592 | bytes 7077892 | tf_op jit(solution)/shard_map/convert_element_type | solution.py:274
  268.4 40.4 %all_to_all.21 = bf16[8,160,1024]{2,1,0:T(8,128)(2,1)S(1)} all-to-all(bf16[8,160,1024]{2,1,0:T(8,128)(2,1)S(1)} %pad_maximum_fusion.1), channel_id=1, replica_groups=mesh['dp_0'=2,'dp_1'=4,'dp_2'=2,'mp_0'=2,'mp_1'=8] {'dp_0','dp_1'}, dimensions={0} | all-to-all | bytes 5242880 | tf_op jit(solution)/shard_map/all_to_all | solution.py:282
  311.4 6.0 %all-to-all-start.3 = ((bf16[16,96,128]{2,1,0:T(8,128)(2,1)}), bf16[16,96,128]{2,1,0:T(8,128)(2,1)}, u32[]{:S(2)}, u32[]{:S(2)}) async-start(bf16[16,96,128]{2,1,0:T(8,128)(2,1)} %pad_maximum_fusion.4), calls=%async_computation.3 | async-start | bytes 786432 | tf_op jit(solution)/shard_map/all_to_all | solution.py:297
  322.0 6.5 %all-to-all-done.3 = bf16[16,96,128]{2,1,0:T(8,128)(2,1)} async-done(((bf16[16,96,128]{2,1,0:T(8,128)(2,1)}), bf16[16,96,128]{2,1,0:T(8,128)(2,1)}, u32[]{:S(2)}, u32[]{:S(2)}) %all-to-all-start.3) | async-done | bytes 393248 | tf_op jit(solution)/shard_map/all_to_all | solution.py:297
  (121 shorter events, 62.1 us)
Async XLA Ops:
  7.2 13.8 %copy-start = (bf16[1024,1024]{1,0:T(8,128)(2,1)S(1)}, bf16[1024,1024]{1,0:T(8,128)(2,1)}, u32[]{:S(2)}) copy-start(bf16[1024,1024]{1,0:T(8,128)(2,1)} %param.20) | copy-start | bytes 6291460
  7.2 86.2 %all-gather.3.cloned.1.call-start = ((), (), s32[]{:S(2)}) async-start(), calls=%async_computation.4 | async-start | bytes 4325376 | tf_op jit(solution)/shard_map/all_gather | solution.py:176
  9.2 238.8 %all-gather.5.cloned.1.call-start = ((), (), s32[]{:S(2)}) async-start(), calls=%async_computation.5 | async-start | bytes 9437184 | tf_op jit(solution)/shard_map/all_gather | solution.py:215
  13.1 3.7 %copy-start.15 = (f32[1,4,768]{2,1,0:T(4,128)S(1)}, f32[1,4,768]{2,1,0:T(4,128)}, u32[]{:S(2)}) copy-start(f32[1,4,768]{2,1,0:T(4,128)} %param.17) | copy-start | bytes 36868
  13.1 3.7 %copy-start.16 = (f32[4,1024]{1,0:T(4,128)S(1)}, f32[4,1024]{1,0:T(4,128)}, u32[]{:S(2)}) copy-start(f32[4,1024]{1,0:T(4,128)} %param.18) | copy-start | bytes 49156
  21.0 12.8 %copy-start.6 = (bf16[1,128,1024]{2,1,0:T(8,128)(2,1)S(1)}, bf16[1,128,1024]{2,1,0:T(8,128)(2,1)}, u32[]{:S(2)}) copy-start(bf16[1,128,1024]{2,1,0:T(8,128)(2,1)} %param.23) | copy-start | bytes 786436
  21.0 17.9 %copy-start.14 = (bf16[1,128,1024]{2,1,0:T(8,128)(2,1)S(1)}, bf16[1,128,1024]{2,1,0:T(8,128)(2,1)}, u32[]{:S(2)}) copy-start(bf16[1,128,1024]{2,1,0:T(8,128)(2,1)} %param.13) | copy-start | bytes 786436
  27.4 11.5 %collective-permute-start.1 = (bf16[128,1024]{1,0:T(8,128)(2,1)S(1)}, bf16[128,1024]{1,0:T(8,128)(2,1)S(1)}, u32[]{:S(2)}, u32[]{:S(2)}) collective-permute-start(bf16[128,1024]{1,0:T(8,128)(2,1)S(1)} %get-tuple-element.36), channel_id=1, source_target_pairs={{1,0},{2,1},{3,2},{4,3},{5,4},{6,5},{7,6},{8,7},{9,8},{10,9},{11,1... | collective-permute-start | bytes 786440 | tf_op jit(solution)/shard_map/ppermute | solution.py:32
  28.7 10.2 %collective-permute-start = (bf16[128,1024]{1,0:T(8,128)(2,1)S(1)}, bf16[128,1024]{1,0:T(8,128)(2,1)S(1)}, u32[]{:S(2)}, u32[]{:S(2)}) collective-permute-start(bf16[128,1024]{1,0:T(8,128)(2,1)S(1)} %get-tuple-element.35), channel_id=1, source_target_pairs={{0,1},{1,2},{2,3},{3,4},{4,5},{5,6},{6,7},{7,8},{8,9},{9,10},{10,1... | collective-permute-start | bytes 786440 | tf_op jit(solution)/shard_map/ppermute | solution.py:32
  33.7 16.7 %collective-permute-start.6 = (bf16[128,1024]{1,0:T(8,128)(2,1)S(1)}, bf16[128,1024]{1,0:T(8,128)(2,1)S(1)}, u32[]{:S(2)}, u32[]{:S(2)}) collective-permute-start(bf16[128,1024]{1,0:T(8,128)(2,1)S(1)} %bitcast.99), channel_id=1, source_target_pairs={{0,8},{8,0},{1,9},{9,1},{2,10},{10,2},{3,11},{11,3},{4,12},{12,4},... | collective-permute-start | bytes 786440 | tf_op jit(solution)/shard_map/ppermute | solution.py:177
  40.3 14.8 %collective-permute-start.2 = (bf16[128,1024]{1,0:T(8,128)(2,1)S(1)}, bf16[128,1024]{1,0:T(8,128)(2,1)S(1)}, u32[]{:S(2)}, u32[]{:S(2)}) collective-permute-start(bf16[128,1024]{1,0:T(8,128)(2,1)S(1)} %multiply_convert_fusion.4), channel_id=1, source_target_pairs={{0,8},{8,0},{1,9},{9,1},{2,10},{10,2},{3,11},{11,3},{4,12},{12,4},... | collective-permute-start | bytes 786440 | tf_op jit(solution)/shard_map/ppermute | solution.py:200
  93.4 11.4 %collective-permute-start.3 = (bf16[4096,512]{1,0:T(8,128)(2,1)}, bf16[4096,512]{1,0:T(8,128)(2,1)}, u32[]{:S(2)}, u32[]{:S(2)}) collective-permute-start(bf16[4096,512]{1,0:T(8,128)(2,1)} %all-gather.3.cloned.1.call-done), channel_id=1, source_target_pairs={{0,16},{16,0},{1,17},{17,1},{2,18},{18,2},{3,19},{19,3},{4,20},{20... | collective-permute-start | bytes 12582920 | tf_op jit(solution)/shard_map/ppermute | solution.py:36
  97.7 10.6 %copy-start.3 = (bf16[4096,512]{1,0:T(8,128)(2,1)S(1)}, bf16[4096,512]{1,0:T(8,128)(2,1)}, u32[]{:S(2)}) copy-start(bf16[4096,512]{1,0:T(8,128)(2,1)} %all-gather.3.cloned.1.call-done) | copy-start | bytes 12582916
  179.2 34.7 %all-to-all-start.1 = ((bf16[16,192,128]{2,1,0:T(8,128)(2,1)}), bf16[16,192,128]{2,1,0:T(8,128)(2,1)}, u32[]{:S(2)}, u32[]{:S(2)}) async-start(bf16[16,192,128]{2,1,0:T(8,128)(2,1)} %get-tuple-element.12), calls=%async_computation.1 | async-start | bytes 1572864 | tf_op jit(solution)/shard_map/all_to_all | solution.py:219
  217.0 8.5 %copy-start.18 = (s32[1,768]{1,0:T(1,128)S(1)}, s32[1,768]{1,0:T(1,128)}, u32[]{:S(2)}) copy-start(s32[1,768]{1,0:T(1,128)} %param.14) | copy-start | bytes 9220
  219.4 16.8 %copy-start.13 = (bf16[128,1024]{1,0:T(8,128)(2,1)}, bf16[128,1024]{1,0:T(8,128)(2,1)S(1)}, u32[]{:S(2)}) copy-start(bf16[128,1024]{1,0:T(8,128)(2,1)S(1)} %subtract_convert_fusion) | copy-start | bytes 786436
  219.5 12.2 %collective-permute-start.5 = (bf16[128,1024]{1,0:T(8,128)(2,1)S(1)}, bf16[128,1024]{1,0:T(8,128)(2,1)S(1)}, u32[]{:S(2)}, u32[]{:S(2)}) collective-permute-start(bf16[128,1024]{1,0:T(8,128)(2,1)S(1)} %subtract_convert_fusion), channel_id=1, source_target_pairs={{1,0},{2,1},{3,2},{4,3},{5,4},{6,5},{7,6},{8,7},{9,8},{10,9},{11,1... | collective-permute-start | bytes 786440 | tf_op jit(solution)/shard_map/ppermute | solution.py:32
  220.8 10.9 %collective-permute-start.4 = (bf16[128,1024]{1,0:T(8,128)(2,1)S(1)}, bf16[128,1024]{1,0:T(8,128)(2,1)}, u32[]{:S(2)}, u32[]{:S(2)}) collective-permute-start(bf16[128,1024]{1,0:T(8,128)(2,1)S(1)} %subtract_convert_fusion), channel_id=1, source_target_pairs={{0,1},{1,2},{2,3},{3,4},{4,5},{5,6},{6,7},{7,8},{8,9},{9,10},{10,1... | collective-permute-start | bytes 786440 | tf_op jit(solution)/shard_map/ppermute | solution.py:32
  256.2 5.9 %copy-start.2 = (bf16[8,2,144,1024]{3,2,1,0:T(8,128)(2,1)}, bf16[8,2,144,1024]{3,2,1,0:T(8,128)(2,1)S(1)}, u32[]{:S(2)}) copy-start(bf16[8,2,144,1024]{3,2,1,0:T(8,128)(2,1)S(1)} %pad_maximum_fusion) | copy-start | bytes 14155780
  256.2 4.2 %copy-start.5 = (f32[768,1024]{1,0:T(8,128)S(1)}, f32[768,1024]{1,0:T(8,128)}, u32[]{:S(2)}) copy-start(f32[768,1024]{1,0:T(8,128)} %copy-done.4) | copy-start | bytes 9437188
  258.0 6.6 %collective-permute-start.7 = (bf16[8,144,1024]{2,1,0:T(8,128)(2,1)}, bf16[8,144,1024]{2,1,0:T(8,128)(2,1)}, u32[]{:S(2)}, u32[]{:S(2)}) collective-permute-start(bf16[8,144,1024]{2,1,0:T(8,128)(2,1)} %dynamic-slice_bitcast_fusion), channel_id=1, source_target_pairs={{0,16},{16,0},{1,17},{17,1},{2,18},{18,2},{3,19},{19,3},{4,20},{20... | collective-permute-start | bytes 7077896 | tf_op jit(solution)/shard_map/ppermute | solution.py:36
  262.1 2.4 collective-permute-start.8
  310.5 20.3 %copy-start.1 = (bf16[1024,1024]{1,0:T(8,128)(2,1)S(1)}, bf16[1024,1024]{1,0:T(8,128)(2,1)}, u32[]{:S(2)}) copy-start(bf16[1024,1024]{1,0:T(8,128)(2,1)} %param.20) | copy-start | bytes 6291460
  311.4 17.1 %all-to-all-start.3 = ((bf16[16,96,128]{2,1,0:T(8,128)(2,1)}), bf16[16,96,128]{2,1,0:T(8,128)(2,1)}, u32[]{:S(2)}, u32[]{:S(2)}) async-start(bf16[16,96,128]{2,1,0:T(8,128)(2,1)} %pad_maximum_fusion.4), calls=%async_computation.3 | async-start | bytes 786432 | tf_op jit(solution)/shard_map/all_to_all | solution.py:297
  (8 other events, 20.8 us)
Sparse Core Ops, SparseCore 0:
  11.2 82.1 all-gather.2
  95.2 133.5 all-gather.4

commit v3 on v2

--- a/solution.py
+++ b/solution.py
@@ -170,10 +170,8 @@
     dest_local = edge_dest[0] - (band - 1) * nodes
 
     width = w_qkv.shape[2]
-    upper = lax.axis_index("dp_0")
     w_rows = jnp.concatenate([w_qkv.transpose(0, 2, 1).reshape(3 * width, channels), w_o], axis=0)
-    w_part = lax.dynamic_slice_in_dim(column_half(w_rows, core), upper * 2 * width, 2 * width, 0)
-    w_mine = lax.all_gather(w_part, ("dp_0",) + MP, axis=0, tiled=True)
+    w_mine = lax.all_gather(column_half(w_rows, core), MP, axis=0, tiled=True)
     cot_beside = lax.ppermute(cot, "mp_0", [(0, 1), (1, 0)])
 
     projected = dot(grid, w_in, NN)
@@ -203,10 +201,9 @@
     both = jnp.concatenate([normed, cot], axis=0)
     heads = dot(column_half(both, core), w_mine, NT) + dot(column_half(both, 1 - core), w_other, NT)
     column = lax.broadcasted_iota(jnp.int32, (nodes, heads.shape[1]), 1)
-    of_output = (column >= 2 * width * bands) & (column % (2 * width) >= width)
+    of_output = column % (4 * width) >= 3 * width
     heads = jnp.where(of_output, heads[nodes:], heads[:nodes]).astype(BF)
-    heads = heads.reshape(nodes, 2, bands, 2 * width).transpose(2, 0, 1, 3)
-    heads = heads.reshape(bands, nodes, 4 * width)
+    heads = heads.reshape(nodes, bands, 4 * width).transpose(1, 0, 2)
     heads = lax.all_to_all(heads, MP, 0, 0, tiled=True).reshape(bands * nodes, 4 * width)
 
     wide = jnp.concatenate([normed, cot], axis=1)
@@ -220,8 +217,7 @@
     pieces = pieces.reshape(bands * 3 * width, nodes)
 
     def only_qkv(rows):
-        rows = rows.reshape(2, bands, 2 * width, -1)
-        rows = jnp.concatenate([rows[0], rows[1, :, :width]], axis=1)
+        rows = rows.reshape(bands, 4 * width, -1)[:, : 3 * width]
         return rows.reshape(bands * 3 * width, -1)
 
     dx = both_halves(

time: 340 us -> 335 us (0.985)
  local copies, waits for them, and re-layouts: 33.6 us -> 16.3 us
  waiting for transfers between devices: 82 us -> 95.2 us
    all_gather x1, waiting for transfers between devices: 37.2 us -> 0.01 us  [shards(): w_mine = lax.all_gather(column_half(w_rows, core), MP, axis=0, tiled=True)]
    ppermute x1, waiting for transfers between devices: 0.01 us -> 21.5 us  [shards(): cot_beside = lax.ppermute(cot, 'mp_0', [(0, 1), (1, 0)])]
    all_to_all x1, waiting for transfers between devices: 19.5 us -> 30 us  [shards(): pieces = lax.all_to_all(pieces, MP, 0, 0, tiled=True)]
    ppermute x4, waiting for transfers between devices: 6.16 us -> 15.3 us  [shifted(): return lax.ppermute(block, axis, route)]
    ppermute x1, waiting for transfers between devices: 4.67 us -> 13.7 us  [shards(): normed_beside = lax.ppermute(normed, 'mp_0', [(0, 1), (1, 0)])]
    slice x2 -> x0, local copies, waits for them, and re-layouts: 6.23 us -> none  [only_qkv(): rows = jnp.concatenate([rows[0], rows[1, :, :width]], axis=1)]
    squeeze x2 -> x0, local copies, waits for them, and re-layouts: 4.65 us -> none  [only_qkv(): rows = jnp.concatenate([rows[0], rows[1, :, :width]], axis=1)]
  transfers between devices with their start and end apart: 13 -> 13, of which waited for: 7 -> 10; matrix products, arithmetic and copies ran while one was open for 20% -> 15% of each run, Pallas kernels for 6% -> 6%
where the time goes in v3:
time: 335 us; the launch traced here: 333 us
  waiting for transfers between devices  95.2 us (28%)
  blocking collectives  83.3 us (25%)
  starting transfers between devices  46.3 us (14%)
  matrix products  38 us (11%)
  Pallas kernels  21 us (6%)
  other arithmetic  18.2 us (5%)
  local copies, waits for them, and re-layouts  16.3 us (5%)
  between operations  15.2 us (5%)
    all_to_all x1, blocking collectives, shards(): lax.all_to_all(heads, MP, 0, 0, tiled=True)  42.6 us
    all_to_all x1, blocking collectives, shards(): pair = lax.all_to_all(pair, GROUP, 0, 0, tiled=True)  40.6 us
    dot_general x12, matrix products, dot(): return lax.dot_general(a, b, dims, preferred_element_type=F32)  36.3 us
    all_to_all x1, waiting for transfers between devices, shards(): pieces = lax.all_to_all(pieces, MP, 0, 0, tiled=True)  30 us
    ppermute x1, waiting for transfers between devices, shards(): cot_beside = lax.ppermute(cot, 'mp_0', [(0, 1), (1, 0)])  21.5 us
    pallas_call x1, Pallas kernels, attend(): pl.pallas_call(functools.partial(attend_kernel, block=block, steps=steps,...  21 us
    ppermute x4, waiting for transfers between devices, shifted(): return lax.ppermute(block, axis, route)  15.3 us
    ppermute x1, waiting for transfers between devices, shards(): normed_beside = lax.ppermute(normed, 'mp_0', [(0, 1), (1, 0)])  13.7 us
  transfers between devices with their start and end apart: 13, of which 10 were waited for; matrix products, arithmetic and copies ran while one was open for 15% of the time, Pallas kernels for 6%

profile of v3, /device:TPU:1, one launch (start us, length us, event | category | flops | bytes accessed | tf_op | source)
XLA Modules:
  0.0 333.5 jit_solution(17257007424187574566)
XLA Ops:
  13.0 3.6 %gather_fusion = f32[768,1024]{1,0:T(8,128)} fusion(f32[256,1024]{1,0:T(8,128)S(1)} %fusion.23, s32[1024]{0:T(1024)S(1)} %pad_clamp_fusion.1), kind=kCustom, calls=%fused_computation | custom fusion | bytes 6294528 | tf_op jit(solution)/shard_map/gather | solution.py:182
  16.8 4.1 %multiply_convert_fusion.1 = bf16[768,1024]{1,0:T(8,128)(2,1)} fusion(f32[768,1024]{1,0:T(8,128)} %gather_fusion, f32[768]{0:T(1024)S(1)} %fusion.38, f32[1024]{0:T(1024)S(1)} %bitcast.113, f32[768]{0:T(1024)S(1)} %get-tuple-element.30, f32[1024]{0:T(1024)S(1)} %bitcast.115, f32[768]{0:T(1024)S(1)} %get-tuple-element.31, f32[1024]{0:T(1024)S(1)} %bitcast.111, ...), kind=kLoop, calls=%fused_computation.13 | loop fusion | flops 11010048 | bytes 4750336 | tf_op jit(solution)/shard_map/convert_element_type | solution.py:183
  20.9 5.1 %fusion.49 = (bf16[384,1024]{1,0:T(8,128)(2,1)S(1)}, f32[384,1024]{1,0:T(8,128)}) fusion(bf16[768,1024]{1,0:T(8,128)(2,1)} %multiply_convert_fusion.1, bf16[1024,1024]{1,0:T(8,128)(2,1)S(1)} %copy-done, s32[768]{0:T(1024)S(1)} %get-tuple-element.53), kind=kOutput, calls=%fused_computation.109 | convolution fusion | flops 2216067072 | bytes 6032384 | tf_op jit(solution)/shard_map/dot_general | solution.py:26
  27.2 5.0 %collective-permute-start = (bf16[128,1024]{1,0:T(8,128)(2,1)S(1)}, bf16[128,1024]{1,0:T(8,128)(2,1)S(1)}, u32[]{:S(2)}, u32[]{:S(2)}) collective-permute-start(bf16[128,1024]{1,0:T(8,128)(2,1)S(1)} %get-tuple-element.35), channel_id=1, source_target_pairs={{0,1},{1,2},{2,3},{3,4},{4,5},{5,6},{6,7},{7,8},{8,9},{9,10},{10,1... | collective-permute-start | bytes 786440 | tf_op jit(solution)/shard_map/ppermute | solution.py:32
  32.3 5.2 %collective-permute-start.6 = (bf16[128,1024]{1,0:T(8,128)(2,1)S(1)}, bf16[128,1024]{1,0:T(8,128)(2,1)S(1)}, u32[]{:S(2)}, u32[]{:S(2)}) collective-permute-start(bf16[128,1024]{1,0:T(8,128)(2,1)S(1)} %bitcast.95), channel_id=1, source_target_pairs={{0,8},{8,0},{1,9},{9,1},{2,10},{10,2},{3,11},{11,3},{4,12},{12,4},... | collective-permute-start | bytes 786440 | tf_op jit(solution)/shard_map/ppermute | solution.py:175
  44.2 8.4 %collective-permute-start.2 = (bf16[128,1024]{1,0:T(8,128)(2,1)S(1)}, bf16[128,1024]{1,0:T(8,128)(2,1)S(1)}, u32[]{:S(2)}, u32[]{:S(2)}) collective-permute-start(bf16[128,1024]{1,0:T(8,128)(2,1)S(1)} %multiply_convert_fusion.4), channel_id=1, source_target_pairs={{0,8},{8,0},{1,9},{9,1},{2,10},{10,2},{3,11},{11,3},{4,12},{12,4},... | collective-permute-start | bytes 786440 | tf_op jit(solution)/shard_map/ppermute | solution.py:198
  52.7 21.5 %collective-permute-done.6 = bf16[128,1024]{1,0:T(8,128)(2,1)S(1)} collective-permute-done((bf16[128,1024]{1,0:T(8,128)(2,1)S(1)}, bf16[128,1024]{1,0:T(8,128)(2,1)S(1)}, u32[]{:S(2)}, u32[]{:S(2)}) %collective-permute-start.6) | collective-permute-done | bytes 262176 | tf_op jit(solution)/shard_map/ppermute | solution.py:175
  74.1 13.7 %collective-permute-done.2 = bf16[128,1024]{1,0:T(8,128)(2,1)S(1)} collective-permute-done((bf16[128,1024]{1,0:T(8,128)(2,1)S(1)}, bf16[128,1024]{1,0:T(8,128)(2,1)S(1)}, u32[]{:S(2)}, u32[]{:S(2)}) %collective-permute-start.2) | collective-permute-done | bytes 262176 | tf_op jit(solution)/shard_map/ppermute | solution.py:198
  88.9 4.4 %collective-permute-start.3 = (bf16[4096,512]{1,0:T(8,128)(2,1)}, bf16[4096,512]{1,0:T(8,128)(2,1)}, u32[]{:S(2)}, u32[]{:S(2)}) collective-permute-start(bf16[4096,512]{1,0:T(8,128)(2,1)} %all-gather.3.cloned.1.call-done), channel_id=1, source_target_pairs={{0,16},{16,0},{1,17},{17,1},{2,18},{18,2},{3,19},{19,3},{4,20},{20... | collective-permute-start | bytes 12582920 | tf_op jit(solution)/shard_map/ppermute | solution.py:36
  93.4 7.1 %collective-permute-done.3 = bf16[4096,512]{1,0:T(8,128)(2,1)} collective-permute-done((bf16[4096,512]{1,0:T(8,128)(2,1)}, bf16[4096,512]{1,0:T(8,128)(2,1)}, u32[]{:S(2)}, u32[]{:S(2)}) %collective-permute-start.3) | collective-permute-done | bytes 4194336 | tf_op jit(solution)/shard_map/ppermute | solution.py:36
  100.5 3.5 %fusion.28 = f32[256,4096]{1,0:T(8,128)S(1)} fusion(bf16[4096,512]{1,0:T(8,128)(2,1)} %collective-permute-done.3, s32[]{:T(128)S(6)} %select_n.65, bf16[128,1024]{1,0:T(8,128)(2,1)S(1)} %multiply_convert_fusion.4, bf16[128,1024]{1,0:T(8,128)(2,1)S(1)} %bitcast.97), kind=kOutput, calls=%fused_computation.65 | convolution fusion | flops 1074266112 | bytes 8912900 | tf_op jit(solution)/shard_map/dot_general | solution.py:26
  105.7 42.6 %all_to_all.20 = bf16[16,128,256]{2,1,0:T(8,128)(2,1)} all-to-all(bf16[16,128,256]{2,1,0:T(8,128)(2,1)S(1)} %bitcast.94), channel_id=1, replica_groups=mesh['dp_0'=2,'dp_1'=4,'dp_2'=2,'mp_0'=2,'mp_1'=8] {'mp_0','mp_1'}, dimensions={0} | all-to-all | bytes 2097152 | tf_op jit(solution)/shard_map/all_to_all | solution.py:207
  148.4 21.0 %attend.1 = (bf16[256,2048]{1,0:T(8,128)(2,1)}, bf16[16,192,128]{2,1,0:T(8,128)(2,1)}) custom-call(s32[1]{0:T(128)} %bitcast.12.half_ref, bf16[2048,256]{1,0:T(8,128)(2,1)} %bitcast.103), custom_call_target="tpu_custom_call" | custom-call | flops 6442450944 | bytes 2621440 | tf_op jit(solution)/shard_map/attend/pallas_call | solution.py:111
  169.4 4.3 %all-to-all-start.1 = ((bf16[16,192,128]{2,1,0:T(8,128)(2,1)}), bf16[16,192,128]{2,1,0:T(8,128)(2,1)}, u32[]{:S(2)}, u32[]{:S(2)}) async-start(bf16[16,192,128]{2,1,0:T(8,128)(2,1)} %get-tuple-element.12), calls=%async_computation.1 | async-start | bytes 1572864 | tf_op jit(solution)/shard_map/all_to_all | solution.py:216
  173.7 30.0 %all-to-all-done.1 = bf16[16,192,128]{2,1,0:T(8,128)(2,1)} async-done(((bf16[16,192,128]{2,1,0:T(8,128)(2,1)}), bf16[16,192,128]{2,1,0:T(8,128)(2,1)}, u32[]{:S(2)}, u32[]{:S(2)}) %all-to-all-start.1) | async-done | bytes 786464 | tf_op jit(solution)/shard_map/all_to_all | solution.py:216
  210.6 4.7 %collective-permute-start.4 = (bf16[128,1024]{1,0:T(8,128)(2,1)S(1)}, bf16[128,1024]{1,0:T(8,128)(2,1)}, u32[]{:S(2)}, u32[]{:S(2)}) collective-permute-start(bf16[128,1024]{1,0:T(8,128)(2,1)S(1)} %subtract_convert_fusion), channel_id=1, source_target_pairs={{0,1},{1,2},{2,3},{3,4},{4,5},{5,6},{6,7},{7,8},{8,9},{9,10},{10,1... | collective-permute-start | bytes 786440 | tf_op jit(solution)/shard_map/ppermute | solution.py:32
  215.3 9.0 %collective-permute-done.5 = bf16[128,1024]{1,0:T(8,128)(2,1)S(1)} collective-permute-done((bf16[128,1024]{1,0:T(8,128)(2,1)S(1)}, bf16[128,1024]{1,0:T(8,128)(2,1)S(1)}, u32[]{:S(2)}, u32[]{:S(2)}) %collective-permute-start.5) | collective-permute-done | bytes 262176 | tf_op jit(solution)/shard_map/ppermute | solution.py:32
  226.3 3.6 %gather_fusion.1 = bf16[768,1024]{1,0:T(8,128)(2,1)} fusion(bf16[384,1024]{1,0:T(8,128)(2,1)S(1)} %pad_maximum_fusion.2, s32[1024]{0:T(1024)S(1)} %pad_clamp_fusion), kind=kCustom, calls=%fused_computation.1 | custom fusion | bytes 3148800 | tf_op jit(solution)/shard_map/gather | solution.py:236
  229.9 5.1 %multiply_multiply_fusion = f32[768,1024]{1,0:T(8,128)S(1)} fusion(bf16[1024,1024]{1,0:T(8,128)(2,1)S(1)} %copy-done, f32[768,1024]{1,0:T(8,128)} %gather_fusion, f32[768]{0:T(1024)S(1)} %fusion.38, f32[1024]{0:T(1024)S(1)} %bitcast.114, f32[768]{0:T(1024)S(1)} %get-tuple-element.30, f32[1024]{0:T(1024)S(1)} %bitcast.116, f32[768]{0:T(1024)S(1)} %get-tuple-element.31, ...), kind=kOutput, calls=%fused_computation.11 | convolution fusion | flops 1626341376 | bytes 9993216 | tf_op jit(solution)/shard_map/dot_general | solution.py:26
  241.6 6.2 %convolution_convert_fusion = bf16[2048,256]{1,0:T(8,128)(2,1)S(1)} fusion(bf16[2048,2048]{1,0:T(8,128)(2,1)} %all-gather.5.cloned.1.call-done, bf16[256,2048]{1,0:T(8,128)(2,1)} %get-tuple-element.14), kind=kOutput, calls=%fused_computation.17 | convolution fusion | flops 2148007936 | bytes 10485760 | tf_op jit(solution)/shard_map/dot_general | solution.py:26
  259.7 3.5 %fusion = bf16[8,144,1024]{2,1,0:T(8,128)(2,1)S(1)} fusion(bf16[8,144,1024]{2,1,0:T(8,128)(2,1)} %collective-permute-done.7, bf16[8,2,144,1024]{3,2,1,0:T(8,128)(2,1)} %copy-done.2, s32[]{:T(128)S(6)} %select_n.71), kind=kLoop, calls=%fused_computation.6 | loop fusion | flops 4718592 | bytes 7077892 | tf_op jit(solution)/shard_map/convert_element_type | solution.py:270
  263.5 40.6 %all_to_all.21 = bf16[8,160,1024]{2,1,0:T(8,128)(2,1)S(1)} all-to-all(bf16[8,160,1024]{2,1,0:T(8,128)(2,1)S(1)} %pad_maximum_fusion.1), channel_id=1, replica_groups=mesh['dp_0'=2,'dp_1'=4,'dp_2'=2,'mp_0'=2,'mp_1'=8] {'dp_0','dp_1'}, dimensions={0} | all-to-all | bytes 5242880 | tf_op jit(solution)/shard_map/all_to_all | solution.py:278
  306.6 6.2 %all-to-all-start.3 = ((bf16[16,96,128]{2,1,0:T(8,128)(2,1)}), bf16[16,96,128]{2,1,0:T(8,128)(2,1)}, u32[]{:S(2)}, u32[]{:S(2)}) async-start(bf16[16,96,128]{2,1,0:T(8,128)(2,1)} %pad_maximum_fusion.4), calls=%async_computation.3 | async-start | bytes 786432 | tf_op jit(solution)/shard_map/all_to_all | solution.py:293
  317.5 6.8 %all-to-all-done.3 = bf16[16,96,128]{2,1,0:T(8,128)(2,1)} async-done(((bf16[16,96,128]{2,1,0:T(8,128)(2,1)}), bf16[16,96,128]{2,1,0:T(8,128)(2,1)}, u32[]{:S(2)}, u32[]{:S(2)}) %all-to-all-start.3) | async-done | bytes 393248 | tf_op jit(solution)/shard_map/all_to_all | solution.py:293
  (112 shorter events, 53.1 us)
Async XLA Ops:
  7.2 13.7 %copy-start = (bf16[1024,1024]{1,0:T(8,128)(2,1)S(1)}, bf16[1024,1024]{1,0:T(8,128)(2,1)}, u32[]{:S(2)}) copy-start(bf16[1024,1024]{1,0:T(8,128)(2,1)} %param.20) | copy-start | bytes 6291460
  7.2 81.7 %all-gather.3.cloned.1.call-start = ((), (), s32[]{:S(2)}) async-start(), calls=%async_computation.4 | async-start | bytes 4456448 | tf_op jit(solution)/shard_map/all_gather | solution.py:174
  9.1 232.5 %all-gather.5.cloned.1.call-start = ((), (), s32[]{:S(2)}) async-start(), calls=%async_computation.5 | async-start | bytes 9437184 | tf_op jit(solution)/shard_map/all_gather | solution.py:212
  13.0 3.7 %copy-start.16 = (s32[1,768]{1,0:T(1,128)S(1)}, s32[1,768]{1,0:T(1,128)}, u32[]{:S(2)}) copy-start(s32[1,768]{1,0:T(1,128)} %param.14) | copy-start | bytes 9220
  13.0 3.7 %copy-start.14 = (f32[1,4,768]{2,1,0:T(4,128)S(1)}, f32[1,4,768]{2,1,0:T(4,128)}, u32[]{:S(2)}) copy-start(f32[1,4,768]{2,1,0:T(4,128)} %param.17) | copy-start | bytes 36868
  13.0 3.7 %copy-start.15 = (f32[4,1024]{1,0:T(4,128)S(1)}, f32[4,1024]{1,0:T(4,128)}, u32[]{:S(2)}) copy-start(f32[4,1024]{1,0:T(4,128)} %param.18) | copy-start | bytes 49156
  20.8 11.4 %copy-start.7 = (bf16[1,128,1024]{2,1,0:T(8,128)(2,1)S(1)}, bf16[1,128,1024]{2,1,0:T(8,128)(2,1)}, u32[]{:S(2)}) copy-start(bf16[1,128,1024]{2,1,0:T(8,128)(2,1)} %param.23) | copy-start | bytes 786436
  20.8 22.0 %copy-start.13 = (bf16[1,128,1024]{2,1,0:T(8,128)(2,1)S(1)}, bf16[1,128,1024]{2,1,0:T(8,128)(2,1)}, u32[]{:S(2)}) copy-start(bf16[1,128,1024]{2,1,0:T(8,128)(2,1)} %param.13) | copy-start | bytes 786436
  25.9 14.8 %collective-permute-start.1 = (bf16[128,1024]{1,0:T(8,128)(2,1)S(1)}, bf16[128,1024]{1,0:T(8,128)(2,1)S(1)}, u32[]{:S(2)}, u32[]{:S(2)}) collective-permute-start(bf16[128,1024]{1,0:T(8,128)(2,1)S(1)} %get-tuple-element.36), channel_id=1, source_target_pairs={{1,0},{2,1},{3,2},{4,3},{5,4},{6,5},{7,6},{8,7},{9,8},{10,9},{11,1... | collective-permute-start | bytes 786440 | tf_op jit(solution)/shard_map/ppermute | solution.py:32
  27.2 15.6 %collective-permute-start = (bf16[128,1024]{1,0:T(8,128)(2,1)S(1)}, bf16[128,1024]{1,0:T(8,128)(2,1)S(1)}, u32[]{:S(2)}, u32[]{:S(2)}) collective-permute-start(bf16[128,1024]{1,0:T(8,128)(2,1)S(1)} %get-tuple-element.35), channel_id=1, source_target_pairs={{0,1},{1,2},{2,3},{3,4},{4,5},{5,6},{6,7},{7,8},{8,9},{9,10},{10,1... | collective-permute-start | bytes 786440 | tf_op jit(solution)/shard_map/ppermute | solution.py:32
  32.3 41.9 %collective-permute-start.6 = (bf16[128,1024]{1,0:T(8,128)(2,1)S(1)}, bf16[128,1024]{1,0:T(8,128)(2,1)S(1)}, u32[]{:S(2)}, u32[]{:S(2)}) collective-permute-start(bf16[128,1024]{1,0:T(8,128)(2,1)S(1)} %bitcast.95), channel_id=1, source_target_pairs={{0,8},{8,0},{1,9},{9,1},{2,10},{10,2},{3,11},{11,3},{4,12},{12,4},... | collective-permute-start | bytes 786440 | tf_op jit(solution)/shard_map/ppermute | solution.py:175
  44.2 43.6 %collective-permute-start.2 = (bf16[128,1024]{1,0:T(8,128)(2,1)S(1)}, bf16[128,1024]{1,0:T(8,128)(2,1)S(1)}, u32[]{:S(2)}, u32[]{:S(2)}) collective-permute-start(bf16[128,1024]{1,0:T(8,128)(2,1)S(1)} %multiply_convert_fusion.4), channel_id=1, source_target_pairs={{0,8},{8,0},{1,9},{9,1},{2,10},{10,2},{3,11},{11,3},{4,12},{12,4},... | collective-permute-start | bytes 786440 | tf_op jit(solution)/shard_map/ppermute | solution.py:198
  88.9 11.5 %collective-permute-start.3 = (bf16[4096,512]{1,0:T(8,128)(2,1)}, bf16[4096,512]{1,0:T(8,128)(2,1)}, u32[]{:S(2)}, u32[]{:S(2)}) collective-permute-start(bf16[4096,512]{1,0:T(8,128)(2,1)} %all-gather.3.cloned.1.call-done), channel_id=1, source_target_pairs={{0,16},{16,0},{1,17},{17,1},{2,18},{18,2},{3,19},{19,3},{4,20},{20... | collective-permute-start | bytes 12582920 | tf_op jit(solution)/shard_map/ppermute | solution.py:36
  93.4 10.6 %copy-start.3 = (bf16[4096,512]{1,0:T(8,128)(2,1)S(1)}, bf16[4096,512]{1,0:T(8,128)(2,1)}, u32[]{:S(2)}) copy-start(bf16[4096,512]{1,0:T(8,128)(2,1)} %all-gather.3.cloned.1.call-done) | copy-start | bytes 12582916
  169.4 34.3 %all-to-all-start.1 = ((bf16[16,192,128]{2,1,0:T(8,128)(2,1)}), bf16[16,192,128]{2,1,0:T(8,128)(2,1)}, u32[]{:S(2)}, u32[]{:S(2)}) async-start(bf16[16,192,128]{2,1,0:T(8,128)(2,1)} %get-tuple-element.12), calls=%async_computation.1 | async-start | bytes 1572864 | tf_op jit(solution)/shard_map/all_to_all | solution.py:216
  209.2 20.6 %copy-start.12 = (bf16[128,1024]{1,0:T(8,128)(2,1)}, bf16[128,1024]{1,0:T(8,128)(2,1)S(1)}, u32[]{:S(2)}) copy-start(bf16[128,1024]{1,0:T(8,128)(2,1)S(1)} %subtract_convert_fusion) | copy-start | bytes 786436
  209.3 15.0 %collective-permute-start.5 = (bf16[128,1024]{1,0:T(8,128)(2,1)S(1)}, bf16[128,1024]{1,0:T(8,128)(2,1)S(1)}, u32[]{:S(2)}, u32[]{:S(2)}) collective-permute-start(bf16[128,1024]{1,0:T(8,128)(2,1)S(1)} %subtract_convert_fusion), channel_id=1, source_target_pairs={{1,0},{2,1},{3,2},{4,3},{5,4},{6,5},{7,6},{8,7},{9,8},{10,9},{11,1... | collective-permute-start | bytes 786440 | tf_op jit(solution)/shard_map/ppermute | solution.py:32
  210.6 14.7 %collective-permute-start.4 = (bf16[128,1024]{1,0:T(8,128)(2,1)S(1)}, bf16[128,1024]{1,0:T(8,128)(2,1)}, u32[]{:S(2)}, u32[]{:S(2)}) collective-permute-start(bf16[128,1024]{1,0:T(8,128)(2,1)S(1)} %subtract_convert_fusion), channel_id=1, source_target_pairs={{0,1},{1,2},{2,3},{3,4},{4,5},{5,6},{6,7},{7,8},{8,9},{9,10},{10,1... | collective-permute-start | bytes 786440 | tf_op jit(solution)/shard_map/ppermute | solution.py:32
  249.8 6.2 %copy-start.2 = (bf16[8,2,144,1024]{3,2,1,0:T(8,128)(2,1)}, bf16[8,2,144,1024]{3,2,1,0:T(8,128)(2,1)S(1)}, u32[]{:S(2)}) copy-start(bf16[8,2,144,1024]{3,2,1,0:T(8,128)(2,1)S(1)} %pad_maximum_fusion) | copy-start | bytes 14155780
  249.8 4.5 %copy-start.6 = (f32[768,1024]{1,0:T(8,128)S(1)}, f32[768,1024]{1,0:T(8,128)}, u32[]{:S(2)}) copy-start(f32[768,1024]{1,0:T(8,128)} %copy-done.5) | copy-start | bytes 9437188
  251.7 8.0 %collective-permute-start.7 = (bf16[8,144,1024]{2,1,0:T(8,128)(2,1)}, bf16[8,144,1024]{2,1,0:T(8,128)(2,1)}, u32[]{:S(2)}, u32[]{:S(2)}) collective-permute-start(bf16[8,144,1024]{2,1,0:T(8,128)(2,1)} %dynamic-slice_bitcast_fusion), channel_id=1, source_target_pairs={{0,16},{16,0},{1,17},{17,1},{2,18},{18,2},{3,19},{19,3},{4,20},{20... | collective-permute-start | bytes 7077896 | tf_op jit(solution)/shard_map/ppermute | solution.py:36
  256.1 3.5 %collective-permute-start.8 = (f32[4,1024]{1,0:T(4,128)S(1)}, f32[4,1024]{1,0:T(4,128)S(1)}, u32[]{:S(2)}, u32[]{:S(2)}) collective-permute-start(f32[4,1024]{1,0:T(4,128)S(1)} %convolution_bitcast_fusion), channel_id=1, source_target_pairs={{0,16},{16,0},{1,17},{17,1},{2,18},{18,2},{3,19},{19,3},{4,20},{20... | collective-permute-start | bytes 49160 | tf_op jit(solution)/shard_map/ppermute | solution.py:36
  305.8 20.8 %copy-start.1 = (bf16[1024,1024]{1,0:T(8,128)(2,1)S(1)}, bf16[1024,1024]{1,0:T(8,128)(2,1)}, u32[]{:S(2)}) copy-start(bf16[1024,1024]{1,0:T(8,128)(2,1)} %param.20) | copy-start | bytes 6291460
  306.6 17.6 %all-to-all-start.3 = ((bf16[16,96,128]{2,1,0:T(8,128)(2,1)}), bf16[16,96,128]{2,1,0:T(8,128)(2,1)}, u32[]{:S(2)}, u32[]{:S(2)}) async-start(bf16[16,96,128]{2,1,0:T(8,128)(2,1)} %pad_maximum_fusion.4), calls=%async_computation.3 | async-start | bytes 786432 | tf_op jit(solution)/shard_map/all_to_all | solution.py:293
  (7 other events, 18.1 us)
Sparse Core Ops, SparseCore 0:
  10.4 73.7 all-gather.2
  89.1 142.2 all-gather.4
